TPU v7x, 32 devices: a whole 2x2x4 slice. The times are simulated.
32 devices in a mesh: grp: 2 (over y), brick: 4 (over z), vec: 2 (over x), sub: 2 (over core).
Axes of the slice: x: 2, y: 2, z: 4, core: 2. Of those that a mesh axis runs over, the one named last changes fastest.
Arguments:
- vectors: float32 [128, 3, 2, 16384], P(('vec', 'sub'), None, None, ('grp', 'brick')), parts along dimension 3, may hold values from -6 to 6
- gauge_links: float32 [3, 3, 3, 2, 16384], P(None, None, None, None, ('grp', 'brick')), parts along dimension 4, may hold values from -1 to 1, as said below
- momenta: int32 [27, 3], replicated, may hold values from -3 to 3
Outputs:
- elementals: float32 [128, 54, 2, 128], P(('vec', 'sub'), 'grp', None, 'brick'), parts along dimension 1
There are 2 independent parts, one for each index of `grp`. A program takes and returns all parts, laid end to end along the dimension named above; an argument that names none is the same for every part. Nothing has to cross between parts.
Inputs may be any that keep to these rules, and one draw needn't show every extreme that they name: Each gauge_links[mu, :, :, :, s] is a unitary 3x3 complex matrix.
All inputs are finite; a program needn't handle non-finite values.
Results may differ from a plain program's by a relative error of at most 0.0049.
Values may be sent and summed in bfloat16 or wider, within the bound.
A program may use at most 128 MiB of HBM per device.

v0:
```python
import functools
import math

import jax
import jax.numpy as jnp
from jax import lax
from jax.experimental import pallas as pl
from jax.experimental.pallas import tpu as pltpu
from jax.sharding import PartitionSpec as P

LY = 64
LZ = 8
ITERS = 2


KAPPA = 0.125


def from_behind(array, axis, by):
    peers = lax.axis_size(axis)
    return lax.ppermute(array, axis, [(i, (i + by) % peers) for i in range(peers)])


def padded_2(array, sides, width):
    for axis, dim in sides:
        peers, length = (lax.axis_size(axis), array.shape[dim])
        up = [(i, (i + 1) % peers) for i in range(peers)]
        down = [(j, i) for i, j in up]
        last = lax.slice_in_dim(array, length - width, length, axis=dim)
        initial = lax.slice_in_dim(array, 0, width, axis=dim)
        before = lax.ppermute(last, axis, up)
        after = lax.ppermute(initial, axis, down)
        array = jnp.concatenate([before, array, after], axis=dim)
    return array


def matrix_apply(matrix, source):
    matrix_real = matrix[:, :, 0][None]
    matrix_imag = matrix[:, :, 1][None]
    source_real = source[:, None, :, 0]
    source_imag = source[:, None, :, 1]
    real_part = jnp.sum(matrix_real * source_real - matrix_imag * source_imag, axis=2)
    imag_part = jnp.sum(matrix_real * source_imag + matrix_imag * source_real, axis=2)
    return jnp.stack([real_part, imag_part], axis=2)


def adjoint(matrix):
    return jnp.stack(
        [jnp.swapaxes(matrix[:, :, 0], 0, 1), -jnp.swapaxes(matrix[:, :, 1], 0, 1)], axis=2
    )


def step_depth(values, offset):
    depth_index = lax.iota(jnp.int32, values.shape[-1]) % LZ
    if offset > 0:
        return jnp.where(
            depth_index == LZ - 1, jnp.roll(values, LZ - 1, -1), jnp.roll(values, -1, -1)
        )
    return jnp.where(depth_index == 0, jnp.roll(values, 1 - LZ, -1), jnp.roll(values, 1, -1))


def step_column(values, offset):
    plane = LY * LZ
    column_index = lax.iota(jnp.int32, values.shape[-1]) // LZ % LY
    if offset > 0:
        return jnp.where(
            column_index == LY - 1, jnp.roll(values, plane - LZ, -1), jnp.roll(values, -LZ, -1)
        )
    return jnp.where(column_index == 0, jnp.roll(values, LZ - plane, -1), jnp.roll(values, LZ, -1))


def laplace_step(center, ahead, behind, here_links, back_links):
    forward = matrix_apply(here_links[0], ahead)
    backward = matrix_apply(adjoint(back_links), behind)
    total = forward + backward
    for direction, stepper in ((1, step_column), (2, step_depth)):
        forward = matrix_apply(here_links[direction], stepper(center, 1))
        backward = matrix_apply(adjoint(stepper(here_links[direction], -1)), stepper(center, -1))
        total = total + (forward + backward)
    return center + KAPPA * (total - 6.0 * center)


def shards(vectors, gauge_links, momenta):
    plane = LY * LZ
    local_sites = vectors.shape[3]
    raw_low = vectors.astype(jnp.bfloat16)
    field = vectors
    x_links = gauge_links[0]
    rim = from_behind(x_links[..., local_sites - plane :], "brick", 1)
    back_links = jnp.concatenate([rim, x_links[..., : local_sites - plane]], axis=3)
    for step in range(ITERS):
        padded = padded_2(field, (("brick", 3),), plane)
        field = laplace_step(
            padded[..., plane : plane + local_sites],
            padded[..., 2 * plane :],
            padded[..., :local_sites],
            gauge_links,
            back_links,
        )
    smeared_low = field.astype(jnp.bfloat16)
    raw_sites, smeared_sites = (
        lax.all_to_all(raw_low, ("vec", "sub"), split_axis=3, concat_axis=0, tiled=True),
        lax.all_to_all(smeared_low, ("vec", "sub"), split_axis=3, concat_axis=0, tiled=True),
    )
    groups = lax.axis_size(("vec", "sub"))
    total_vec = raw_sites.shape[0]
    width = raw_sites.shape[3]
    total_x = lax.axis_size("brick") * (local_sites // plane)
    first_site = lax.axis_index("brick") * local_sites + lax.axis_index(("vec", "sub")) * width
    site = first_site + lax.iota(jnp.int32, width)
    layer_index = (site // plane)[None]
    column_index = (site // LZ % LY)[None]
    depth_index = (site % LZ)[None]
    fraction = (
        jnp.mod(momenta[:, 0:1] * layer_index, total_x).astype(jnp.float32) / total_x
        + jnp.mod(momenta[:, 1:2] * column_index, LY).astype(jnp.float32) / LY
        + jnp.mod(momenta[:, 2:3] * depth_index, LZ).astype(jnp.float32) / LZ
    )
    angle = 2.0 * math.pi * fraction
    cosines = jnp.cos(angle)
    sines = jnp.sin(angle)
    right = smeared_sites.reshape((total_vec, 6 * width))
    scale = (3.0 * total_x * plane) ** (-0.5)

    def one_momentum(angles):
        cosine, sine = angles
        real_part = raw_sites[:, :, 0] * cosine - raw_sites[:, :, 1] * sine
        imag_part = raw_sites[:, :, 0] * sine + raw_sites[:, :, 1] * cosine
        phased = jnp.stack([real_part, imag_part], axis=2).astype(jnp.bfloat16)
        turned = jnp.stack([-phased[:, :, 1], phased[:, :, 0]], axis=2)
        left = jnp.concatenate(
            [
                phased.reshape((lax.axis_size(("vec", "sub")) * (total_vec // groups), 6 * width)),
                turned.reshape((lax.axis_size(("vec", "sub")) * (total_vec // groups), 6 * width)),
            ],
            axis=0,
        )
        product = lax.dot_general(
            left, right, (((1,), (1,)), ((), ())), preferred_element_type=jnp.float32
        )
        return product.reshape(
            (2, lax.axis_size(("vec", "sub")) * (total_vec // groups), total_vec)
        )

    blocks = lax.map(one_momentum, (cosines, sines))
    shares = lax.psum_scatter(
        jnp.transpose(blocks, (2, 0, 1, 3)) * scale, ("vec", "sub"), scatter_dimension=0, tiled=True
    )
    return lax.psum_scatter(shares, "brick", scatter_dimension=3, tiled=True)


def smear_kernel(planes, rows, x_ref, lo_ref, hi_ref, lk_ref, out_ref, stage, table, f0, f1, moved_even, moved_odd):
    plane = LY * LZ
    f32 = jnp.float32
    blocks = rows // 8
    depth = lax.broadcasted_iota(jnp.int32, (8, 128), 1) % LZ
    link_depth = lax.broadcasted_iota(jnp.int32, (stage.shape[1], plane), 1) % LZ

    for k in range(6):
        f0[k] = lo_ref[k].astype(f32)
        f0[6 + 3 * planes + k] = hi_ref[k].astype(f32)

    def take(k, carry):
        f0[6 + k] = x_ref[k]
        return carry

    lax.fori_loop(0, 3 * planes, take, 0)
    for j in range(stage.shape[1] // rows):
        at = slice(j * rows, (j + 1) * rows)
        stage[0, at] = lo_ref[6 + j, :, 0:plane].astype(f32)
        stage[1, at] = lo_ref[6 + j, :, plane:].astype(f32)
        stage[2 + planes, at] = hi_ref[6 + j, :, 0:plane].astype(f32)
    for k in range(planes):
        stage[2 + k, 0:54] = lk_ref[:, k * plane : (k + 1) * plane]

    def spread(t, carry):
        here = stage[t + 1]
        behind_x = stage[t]
        behind_y = pltpu.roll(here, LZ, 1)
        behind_z = jnp.where(
            link_depth == 0, pltpu.roll(here, plane - (LZ - 1), 1), pltpu.roll(here, 1, 1)
        )
        for r in range(54):
            table[t, r] = jnp.broadcast_to(here[r : r + 1], (8, plane))
            back = (behind_x, behind_y, behind_z)[r // 18]
            table[t, 54 + r] = jnp.broadcast_to(back[r : r + 1], (8, plane))
        return carry

    lax.fori_loop(0, planes + 2, spread, 0)

    half_blocks = blocks // 2

    def shift(source, at, k, moved):
        rows_at = pl.ds(pl.multiple_of(k % blocks * 8, 8), 8)
        first_lane = k // blocks * plane
        lanes = pl.ds(pl.multiple_of(first_lane, plane), plane)
        for c in range(3):
            v = source[at * 3 + c, rows_at, lanes]
            moved[0, c, rows_at, lanes] = pltpu.roll(v, plane - LZ, 1)
            moved[1, c, rows_at, lanes] = pltpu.roll(v, LZ, 1)
            for part in range(plane // 128):
                w = v[:, part * 128 : part * 128 + 128]
                here = pl.ds(pl.multiple_of(first_lane + part * 128, 128), 128)
                moved[2, c, rows_at, here] = jnp.where(
                    depth == LZ - 1, pltpu.roll(w, LZ - 1, 1), pltpu.roll(w, 127, 1)
                )
                moved[3, c, rows_at, here] = jnp.where(
                    depth == 0, pltpu.roll(w, 128 - (LZ - 1), 1), pltpu.roll(w, 1, 1)
                )

    def block(source, at, links, target, to, k, moved):
        lane, first = k // half_blocks, k % half_blocks * 16
        lanes = (
            pl.ds(pl.multiple_of(lane * 128, 128), 128),
            pl.ds(pl.multiple_of(plane + lane * 128, 128), 128),
        )
        at_rows = [pl.ds(pl.multiple_of(first + 8 * b, 8), 8) for b in range(2)]
        acc = {}

        def add(b, r, part, value):
            acc[b, r, part] = value + acc[b, r, part] if (b, r, part) in acc else value

        for way in range(6):
            direction, back = way // 2, way % 2
            for c in range(3):
                fields = []
                for b in range(2):
                    if direction == 0:
                        index = (at + 1 - 2 * back) * 3 + c
                        fields.append([source[index, at_rows[b], lanes[part]] for part in range(2)])
                    else:
                        fields.append([moved[way - 2, c, at_rows[b], lanes[part]] for part in range(2)])
                for r in range(3):
                    row = direction * 18 + (54 + c * 6 + r * 2 if back else r * 6 + c * 2)
                    ur = table[links, row, :, lanes[0]]
                    ui = table[links, row + 1, :, lanes[0]]
                    for b, (sr, si) in enumerate(fields):
                        if back:
                            add(b, r, 0, ur * sr + ui * si)
                            add(b, r, 1, ur * si - ui * sr)
                        else:
                            add(b, r, 0, ur * sr - ui * si)
                            add(b, r, 1, ur * si + ui * sr)
        for (b, r, part), value in acc.items():
            mid = source[at * 3 + r, at_rows[b], lanes[part]]
            target[to * 3 + r, at_rows[b], lanes[part]] = mid + KAPPA * (value - 6.0 * mid)

    def sweep(source, offset, target, count):
        trips = 2 * blocks

        def begin(k, carry):
            shift(source, 1, k, moved_even)
            return carry

        lax.fori_loop(0, trips, begin, 0)

        def one(t, now, later):
            following = jnp.minimum(t + 1, count - 1) + 1

            def trip(k, carry):
                shift(source, following, k, later)
                block(source, t + 1, t + offset, target, t, k, now)
                return carry

            lax.fori_loop(0, trips, trip, 0)

        def two(h, carry):
            one(2 * h, moved_even, moved_odd)
            one(2 * h + 1, moved_odd, moved_even)
            return carry

        lax.fori_loop(0, count // 2, two, 0)
        if count % 2:
            one(count - 1, moved_even, moved_odd)

    sweep(f0, 0, f1, planes + 2)
    sweep(f1, 1, f0, planes)

    def put(k, carry):
        out_ref[k] = f0[k].astype(out_ref.dtype)
        return carry

    lax.fori_loop(0, 3 * planes, put, 0)


def product_kernel(groups, rows, count, scale, order_ref, cos_ref, sin_ref, smeared_ref, *rest):
    plane = LY * LZ
    raw_refs = rest[:groups]
    out_refs = rest[groups : 2 * groups]
    sides = (rest[2 * groups : 2 * groups + 2], rest[2 * groups + 2 : 2 * groups + 4])
    total = rest[2 * groups + 4]
    chunks = smeared_ref.shape[0]
    total[...] = jnp.zeros_like(total)
    per = max(1, 256 // rows)

    def fill(k, right):
        for u in range(groups):
            raw = raw_refs[u][k]
            first = 2 * rows * u
            right[first : first + rows, :] = raw
            right[first + rows : first + 2 * rows, 0:plane] = -raw[:, plane:]
            right[first + rows : first + 2 * rows, plane:] = raw[:, :plane]

    def turn(k, left, q):
        for lane in range(0, plane, 128):
            cosine = cos_ref[k // 3, q : q + 1, lane : lane + 128]
            sine = sin_ref[k // 3, q : q + 1, lane : lane + 128]
            for row in range(0, rows, 16):
                sr = smeared_ref[k, row : row + 16, lane : lane + 128].astype(jnp.float32)
                si = smeared_ref[k, row : row + 16, plane + lane : plane + lane + 128].astype(jnp.float32)
                at = slice(q * rows + row, q * rows + row + 16)
                left[at, lane : lane + 128] = (cosine * sr + sine * si).astype(left.dtype)
                left[at, plane + lane : plane + lane + 128] = (cosine * si - sine * sr).astype(left.dtype)

    def stage(k, side, later, other):
        right, left = side
        for q0 in range(0, count, per):
            q1 = min(q0 + per, count)
            at = slice(q0 * rows, q1 * rows)
            part = lax.dot_general(
                right[...], left[at, :], (((1,), (1,)), ((), ())), preferred_element_type=jnp.float32
            )
            for q in range(q0, q1):
                turn(later, other[1], q)
            total[:, at] += part
        fill(later, other[0])

    fill(0, sides[0][0])
    for q in range(count):
        turn(0, sides[0][1], q)

    def two(h, carry):
        k = 2 * h
        stage(k, sides[0], jnp.minimum(k + 1, chunks - 1), sides[1])
        stage(k + 1, sides[1], jnp.minimum(k + 2, chunks - 1), sides[0])
        return carry

    lax.fori_loop(0, chunks // 2, two, 0)
    if chunks % 2:
        stage(chunks - 1, sides[0], chunks - 1, sides[1])
    for k in range(groups):
        first = pl.multiple_of(order_ref[k] * (2 * rows), 2 * rows)
        out_refs[k][...] = (total[pl.ds(first, 2 * rows), :] * scale).astype(out_refs[k].dtype)


def phase_tables(momenta, local_sites, total_x):
    plane = LY * LZ
    site = lax.axis_index("brick") * local_sites + lax.iota(jnp.int32, local_sites)
    site = site.reshape((local_sites // plane, 1, plane))
    fraction = (
        jnp.mod(momenta[None, :, 0:1] * (site // plane), total_x).astype(jnp.float32) / total_x
        + jnp.mod(momenta[None, :, 1:2] * (site // LZ % LY), LY).astype(jnp.float32) / LY
        + jnp.mod(momenta[None, :, 2:3] * (site % LZ), LZ).astype(jnp.float32) / LZ
    )
    angle = 2.0 * math.pi * fraction
    return jnp.cos(angle), jnp.sin(angle)


def shards_kernels(vectors, gauge_links, momenta):
    plane = LY * LZ
    rows, local_sites = vectors.shape[0], vectors.shape[3]
    planes = local_sites // plane
    bricks, vecs, subs = (lax.axis_size(a) for a in ("brick", "vec", "sub"))
    groups = vecs * subs
    count = momenta.shape[0]
    low = jnp.bfloat16
    wide = jnp.transpose(vectors.reshape((rows, 3, 2, planes, plane)), (3, 1, 0, 2, 4))
    wide = wide.reshape((planes * 3, rows, 2 * plane))
    raw = wide.astype(low)
    links = gauge_links.reshape((54, local_sites))
    fold = -(-54 // rows)

    def with_links(part, piece):
        piece = jnp.pad(piece.astype(low), ((0, fold * rows - 54), (0, 0)))
        return jnp.concatenate([part, piece.reshape((fold, rows, 2 * plane))], axis=0)

    below = from_behind(with_links(raw[-6:], links[:, -2 * plane :]), "brick", 1)
    above = from_behind(with_links(raw[:6], links[:, : 2 * plane]), "brick", -1)
    across = [raw] + [from_behind(raw, "vec", -kv) for kv in range(1, vecs)]
    cosines, sines = phase_tables(momenta, local_sites, bricks * planes)

    vmem = pl.BlockSpec(memory_space=pltpu.VMEM)
    smeared = pl.pallas_call(
        functools.partial(smear_kernel, planes, rows),
        out_shape=jax.ShapeDtypeStruct((planes * 3, rows, 2 * plane), low),
        in_specs=[vmem] * 4,
        out_specs=vmem,
        scratch_shapes=[
            pltpu.VMEM((planes + 3, fold * rows, plane), jnp.float32),
            pltpu.VMEM((planes + 2, 108, 8, plane), jnp.float32),
            pltpu.VMEM(((planes + 4) * 3, rows, 2 * plane), jnp.float32),
            pltpu.VMEM(((planes + 2) * 3, rows, 2 * plane), jnp.float32),
            pltpu.VMEM((4, 3, rows, 2 * plane), jnp.float32),
            pltpu.VMEM((4, 3, rows, 2 * plane), jnp.float32),
        ],
        compiler_params=pltpu.CompilerParams(vmem_limit_bytes=48 * 2**20),
        cost_estimate=pl.CostEstimate(
            flops=432 * 2 * (planes + 1) * plane * rows * 4, bytes_accessed=4 * 2**20, transcendentals=0
        ),
        name="smear",
    )(wide, below, above, links)
    *across, smeared = lax.optimization_barrier((*across, smeared))
    gathered = []
    for one in across:
        for ks in range(subs):
            gathered.append(one if ks == 0 else from_behind(one, "sub", -ks))

    me_vec, me_sub, me_brick = (lax.axis_index(a) for a in ("vec", "sub", "brick"))
    owner = (me_brick + lax.iota(jnp.int32, groups)) % groups
    order = (owner // subs - me_vec) % vecs * subs + (owner % subs - me_sub) % subs
    scale = (3.0 * bricks * local_sites) ** (-0.5)
    blocks = pl.pallas_call(
        functools.partial(product_kernel, groups, rows, count, scale),
        out_shape=[jax.ShapeDtypeStruct((2 * rows, count * rows), low)] * groups,
        in_specs=[pl.BlockSpec(memory_space=pltpu.SMEM)] + [vmem] * (3 + groups),
        out_specs=[vmem] * groups,
        scratch_shapes=[
            pltpu.VMEM((2 * rows * groups, 2 * plane), low),
            pltpu.VMEM((count * rows, 2 * plane), low),
            pltpu.VMEM((2 * rows * groups, 2 * plane), low),
            pltpu.VMEM((count * rows, 2 * plane), low),
            pltpu.VMEM((2 * rows * groups, count * rows), jnp.float32),
        ],
        compiler_params=pltpu.CompilerParams(vmem_limit_bytes=40 * 2**20),
        cost_estimate=pl.CostEstimate(
            flops=2 * 2 * rows * groups * count * rows * 6 * local_sites,
            bytes_accessed=8 * 2**20,
            transcendentals=0,
        ),
        name="product",
    )(order, cosines, sines, smeared, *gathered)

    total = None
    for k in range(groups):
        pairs = [
            (b * groups + u, u * groups + (b + k) % groups)
            for b in range(bricks)
            for u in range(groups)
        ]
        got = lax.ppermute(blocks[k], ("brick", "vec", "sub"), pairs).astype(jnp.float32)
        total = got if total is None else total + got
    return jnp.transpose(total.reshape((2, rows, count, rows)), (1, 2, 0, 3))


def choose(vectors, gauge_links, momenta):
    groups = lax.axis_size(("vec", "sub"))
    planes = vectors.shape[3] // (LY * LZ)
    if groups == lax.axis_size("brick") and planes >= 2 and vectors.shape[0] % 16 == 0:
        return shards_kernels(vectors, gauge_links, momenta)
    return shards(vectors, gauge_links, momenta)


def solution(mesh):
    in_specs = (
        P(("vec", "sub"), None, None, ("grp", "brick")),
        P(None, None, None, None, ("grp", "brick")),
        P(),
    )
    out_specs = P(("vec", "sub"), "grp", None, "brick")
    return jax.shard_map(choose, mesh=mesh, in_specs=in_specs, out_specs=out_specs, check_vma=False)
```

profile of v0, /device:TPU:1, one launch (start us, length us, event | category | flops | bytes accessed | tf_op | source)
XLA Modules:
  0.0 98.4 jit_solution(2390186226981511379)
XLA Ops:
  0.0 2.9 %reshape.170 = f32[32,3,2,4,512]{4,3,2,1,0:T(4,128)S(1)} reshape(f32[32,3,2,2048]{3,2,1,0:T(2,128)} %param.3) | data formatting | bytes 3145728 | tf_op jit(solution)/shard_map/reshape | solution.py:367
  2.9 0.8 copy.9
  3.7 1.4 %reshape.171.x_ref = f32[12,32,1024]{2,1,0:T(8,128)S(1)} reshape(f32[4,3,32,2,512]{4,3,2,1,0:T(2,128)S(1)} %bitcast.12) | data formatting | bytes 3145728 | tf_op jit(solution)/shard_map/reshape | solution.py:368
  5.1 0.1 convert_element_type.32.rest_0_
  5.2 2.1 %collective-permute-start = (bf16[12,32,1024]{2,1,0:T(8,128)(2,1)S(1)}, bf16[12,32,1024]{2,1,0:T(8,128)(2,1)}, u32[]{:S(2)}, u32[]{:S(2)}) collective-permute-start(bf16[12,32,1024]{2,1,0:T(8,128)(2,1)S(1)} %convert_element_type.32.rest_0_), channel_id=1, source_target_pairs={{0,2},{2,0},{1,3},{3,1},{4,6},{6,4},{5,7},{7,5},{8,10},{10,8},{9,1... | collective-permute-start | bytes 2359304 | tf_op jit(solution)/shard_map/ppermute | solution.py:21
  7.3 0.8 fusion.23
  8.1 1.3 %reshape.172.lk_ref = f32[54,2048]{1,0:T(8,128)S(1)} reshape(f32[3,3,3,2,2048]{4,3,2,1,0:T(2,128)} %param.4) | data formatting | bytes 884736 | tf_op jit(solution)/shard_map/reshape | solution.py:370
  9.5 0.0 copy-start
  9.5 0.8 pad_maximum_fusion
  10.4 1.3 %collective-permute-start.1 = (bf16[8,32,1024]{2,1,0:T(8,128)(2,1)}, bf16[8,32,1024]{2,1,0:T(8,128)(2,1)S(1)}, u32[]{:S(2)}, u32[]{:S(2)}) collective-permute-start(bf16[8,32,1024]{2,1,0:T(8,128)(2,1)} %pad_maximum_fusion), channel_id=1, source_target_pairs={{0,4},{4,8},{8,12},{12,0},{1,5},{5,9},{9,13},{13,1},{2,6},{6,10},{... | collective-permute-start | bytes 1572872 | tf_op jit(solution)/shard_map/ppermute | solution.py:21
  11.7 0.0 copy-done
  11.7 0.9 pad_maximum_fusion.1
  12.6 2.1 %collective-permute-start.2 = (bf16[8,32,1024]{2,1,0:T(8,128)(2,1)}, bf16[8,32,1024]{2,1,0:T(8,128)(2,1)}, u32[]{:S(2)}, u32[]{:S(2)}) collective-permute-start(bf16[8,32,1024]{2,1,0:T(8,128)(2,1)} %pad_maximum_fusion.1), channel_id=1, source_target_pairs={{0,12},{4,0},{8,4},{12,8},{1,13},{5,1},{9,5},{13,9},{2,14},{6,2},{... | collective-permute-start | bytes 1572872 | tf_op jit(solution)/shard_map/ppermute | solution.py:21
  14.6 0.0 copy-start.1
  14.6 10.4 %collective-permute-done.1.lo_ref = bf16[8,32,1024]{2,1,0:T(8,128)(2,1)S(1)} collective-permute-done((bf16[8,32,1024]{2,1,0:T(8,128)(2,1)}, bf16[8,32,1024]{2,1,0:T(8,128)(2,1)S(1)}, u32[]{:S(2)}, u32[]{:S(2)}) %collective-permute-start.1) | collective-permute-done | bytes 524320 | tf_op jit(solution)/shard_map/ppermute | solution.py:21
  25.1 12.6 %collective-permute-done.2.hi_ref = bf16[8,32,1024]{2,1,0:T(8,128)(2,1)} collective-permute-done((bf16[8,32,1024]{2,1,0:T(8,128)(2,1)}, bf16[8,32,1024]{2,1,0:T(8,128)(2,1)}, u32[]{:S(2)}, u32[]{:S(2)}) %collective-permute-start.2) | collective-permute-done | bytes 524320 | tf_op jit(solution)/shard_map/ppermute | solution.py:21
  37.6 17.7 %smear.1.smeared_ref = bf16[12,32,1024]{2,1,0:T(8,128)(2,1)S(1)} custom-call(f32[12,32,1024]{2,1,0:T(8,128)S(1)} %reshape.171.x_ref, bf16[8,32,1024]{2,1,0:T(8,128)(2,1)S(1)} %collective-permute-done.1.lo_ref, bf16[8,32,1024]{2,1,0:T(8,128)(2,1)} %collective-permute-done.2.hi_ref, f32[54,2048]{1,0:T(8,128)S(1)} %reshape.172.lk_ref), custom_call_target="tpu_custom_call" | custom-call | flops 283115520 | bytes 4194304 | tf_op jit(solution)/shard_map/smear/pallas_call | solution.py:383
  55.4 0.0 collective-permute-done.rest_2_
  55.4 0.6 collective-permute-start.3
  56.0 0.1 collective-permute-start.4
  56.1 0.0 copy-done.1
  56.1 1.4 %fusion.12 = (f32[4,27,512]{2,1,0:T(8,128)S(1)}, f32[4,27,512]{2,1,0:T(8,128)S(1)}) fusion(s32[4,512]{1,0:T(4,128)S(1)} %get-tuple-element.28, s32[27]{0:T(128)S(1)} %get-tuple-element.26, s32[4,512]{1,0:T(4,128)S(1)} %get-tuple-element.29, s32[27]{0:T(128)S(1)} %get-tuple-element.27, s32[4,512]{1,0:T(4,128)S(1)} %add_select_fusion.6, ...), kind=kLoop, calls=%fused_computation.31 | loop fusion | flops 2488320 | bytes 467268 | tf_op jit(solution)/shard_map/sin | solution.py:356
  57.5 0.4 collective-permute-done.3.rest_1_
  57.9 1.1 %collective-permute-done.4.rest_3_ = bf16[12,32,1024]{2,1,0:T(8,128)(2,1)S(1)} collective-permute-done((bf16[12,32,1024]{2,1,0:T(8,128)(2,1)}, bf16[12,32,1024]{2,1,0:T(8,128)(2,1)S(1)}, u32[]{:S(2)}, u32[]{:S(2)}) %collective-permute-start.4) | collective-permute-done | bytes 786464 | tf_op jit(solution)/shard_map/ppermute | solution.py:21
  59.0 13.1 %product.1 = (bf16[64,864]{1,0:T(8,128)(2,1)S(1)}, bf16[64,864]{1,0:T(8,128)(2,1)S(1)}, bf16[64,864]{1,0:T(8,128)(2,1)S(1)}, bf16[64,864]{1,0:T(8,128)(2,1)S(1)}) custom-call(s32[4]{0:T(128)S(1)} %fusion.17.order_ref, f32[4,27,512]{2,1,0:T(8,128)S(1)} %get-tuple-element.24.cos_ref, f32[4,27,512]{2,1,0:T(8,128)S(1)} %get-tuple-element.23.sin_ref, ...), custom_call_target="tpu_custom_call" | custom-call | flops 5435817984 | bytes 8388608 | tf_op jit(solution)/shard_map/product/pallas_call | solution.py:412
  72.1 2.5 %collective-permute-start.5 = (bf16[64,864]{1,0:T(8,128)(2,1)S(1)}, bf16[64,864]{1,0:T(8,128)(2,1)S(1)}, u32[]{:S(2)}, u32[]{:S(2)}) collective-permute-start(bf16[64,864]{1,0:T(8,128)(2,1)S(1)} %get-tuple-element.15), channel_id=1, source_target_pairs={{0,0},{1,4},{2,8},{3,12},{4,1},{5,5},{6,9},{7,13},{8,2},{9,6},{10,... | collective-permute-start | bytes 331784 | tf_op jit(solution)/shard_map/ppermute | solution.py:440
  74.6 0.1 collective-permute-start.6
  74.6 1.3 %collective-permute-start.7 = (bf16[64,864]{1,0:T(8,128)(2,1)S(1)}, bf16[64,864]{1,0:T(8,128)(2,1)S(1)}, u32[]{:S(2)}, u32[]{:S(2)}) collective-permute-start(bf16[64,864]{1,0:T(8,128)(2,1)S(1)} %get-tuple-element.17), channel_id=1, source_target_pairs={{0,2},{1,6},{2,10},{3,14},{4,3},{5,7},{6,11},{7,15},{8,0},{9,4},{1... | collective-permute-start | bytes 331784 | tf_op jit(solution)/shard_map/ppermute | solution.py:440
  76.0 3.1 %collective-permute-start.8 = (bf16[64,864]{1,0:T(8,128)(2,1)S(1)}, bf16[64,864]{1,0:T(8,128)(2,1)S(1)}, u32[]{:S(2)}, u32[]{:S(2)}) collective-permute-start(bf16[64,864]{1,0:T(8,128)(2,1)S(1)} %get-tuple-element.18), channel_id=1, source_target_pairs={{0,3},{1,7},{2,11},{3,15},{4,0},{5,4},{6,8},{7,12},{8,1},{9,5},{10... | collective-permute-start | bytes 331784 | tf_op jit(solution)/shard_map/ppermute | solution.py:440
  79.1 0.0 collective-permute-done.5
  79.1 0.0 collective-permute-done.6
  79.1 7.0 %collective-permute-done.7 = bf16[64,864]{1,0:T(8,128)(2,1)S(1)} collective-permute-done((bf16[64,864]{1,0:T(8,128)(2,1)S(1)}, bf16[64,864]{1,0:T(8,128)(2,1)S(1)}, u32[]{:S(2)}, u32[]{:S(2)}) %collective-permute-start.7) | collective-permute-done | bytes 110624 | tf_op jit(solution)/shard_map/ppermute | solution.py:440
  86.0 10.3 %collective-permute-done.8 = bf16[64,864]{1,0:T(8,128)(2,1)S(1)} collective-permute-done((bf16[64,864]{1,0:T(8,128)(2,1)S(1)}, bf16[64,864]{1,0:T(8,128)(2,1)S(1)}, u32[]{:S(2)}, u32[]{:S(2)}) %collective-permute-start.8) | collective-permute-done | bytes 110624 | tf_op jit(solution)/shard_map/ppermute | solution.py:440
  96.3 0.1 convert_add_fusion
  96.4 0.4 reshape.175
  96.8 1.6 %copy.7 = f32[32,27,2,32]{3,2,1,0:T(2,128)} copy(f32[32,27,2,32]{3,1,0,2:T(8,128)S(1)} %bitcast.13) | data formatting | bytes 442368 | tf_op jit(solution)/shard_map/transpose | solution.py:442
  (8 shorter events, 0.1 us)
Async XLA Ops:
  5.2 50.2 %collective-permute-start = (bf16[12,32,1024]{2,1,0:T(8,128)(2,1)S(1)}, bf16[12,32,1024]{2,1,0:T(8,128)(2,1)}, u32[]{:S(2)}, u32[]{:S(2)}) collective-permute-start(bf16[12,32,1024]{2,1,0:T(8,128)(2,1)S(1)} %convert_element_type.32.rest_0_), channel_id=1, source_target_pairs={{0,2},{2,0},{1,3},{3,1},{4,6},{6,4},{5,7},{7,5},{8,10},{10,8},{9,1... | collective-permute-start | bytes 2359304 | tf_op jit(solution)/shard_map/ppermute | solution.py:21
  9.5 2.2 %copy-start = (bf16[6,32,1024]{2,1,0:T(8,128)(2,1)S(1)}, bf16[6,32,1024]{2,1,0:T(8,128)(2,1)}, u32[]{:S(2)}) copy-start(bf16[6,32,1024]{2,1,0:T(8,128)(2,1)} %get-tuple-element.19) | copy-start | bytes 1179652
  10.4 14.7 %collective-permute-start.1 = (bf16[8,32,1024]{2,1,0:T(8,128)(2,1)}, bf16[8,32,1024]{2,1,0:T(8,128)(2,1)S(1)}, u32[]{:S(2)}, u32[]{:S(2)}) collective-permute-start(bf16[8,32,1024]{2,1,0:T(8,128)(2,1)} %pad_maximum_fusion), channel_id=1, source_target_pairs={{0,4},{4,8},{8,12},{12,0},{1,5},{5,9},{9,13},{13,1},{2,6},{6,10},{... | collective-permute-start | bytes 1572872 | tf_op jit(solution)/shard_map/ppermute | solution.py:21
  12.6 25.1 %collective-permute-start.2 = (bf16[8,32,1024]{2,1,0:T(8,128)(2,1)}, bf16[8,32,1024]{2,1,0:T(8,128)(2,1)}, u32[]{:S(2)}, u32[]{:S(2)}) collective-permute-start(bf16[8,32,1024]{2,1,0:T(8,128)(2,1)} %pad_maximum_fusion.1), channel_id=1, source_target_pairs={{0,12},{4,0},{8,4},{12,8},{1,13},{5,1},{9,5},{13,9},{2,14},{6,2},{... | collective-permute-start | bytes 1572872 | tf_op jit(solution)/shard_map/ppermute | solution.py:21
  14.6 41.5 %copy-start.1 = (s32[27,3]{0,1:T(4,128)S(1)}, s32[27,3]{0,1:T(4,128)}, u32[]{:S(2)}) copy-start(s32[27,3]{0,1:T(4,128)} %param.5) | copy-start | bytes 976
  55.4 2.5 %collective-permute-start.3 = (bf16[12,32,1024]{2,1,0:T(8,128)(2,1)S(1)}, bf16[12,32,1024]{2,1,0:T(8,128)(2,1)S(1)}, u32[]{:S(2)}, u32[]{:S(2)}) collective-permute-start(bf16[12,32,1024]{2,1,0:T(8,128)(2,1)S(1)} %convert_element_type.32.rest_0_), channel_id=1, source_target_pairs={{0,1},{1,0},{2,3},{3,2},{4,5},{5,4},{6,7},{7,6},{8,9},{9,8},{10,11... | collective-permute-start | bytes 2359304 | tf_op jit(solution)/shard_map/ppermute | solution.py:21
  56.0 3.0 %collective-permute-start.4 = (bf16[12,32,1024]{2,1,0:T(8,128)(2,1)}, bf16[12,32,1024]{2,1,0:T(8,128)(2,1)S(1)}, u32[]{:S(2)}, u32[]{:S(2)}) collective-permute-start(bf16[12,32,1024]{2,1,0:T(8,128)(2,1)} %collective-permute-done.rest_2_), channel_id=1, source_target_pairs={{0,1},{1,0},{2,3},{3,2},{4,5},{5,4},{6,7},{7,6},{8,9},{9,8},{10,11... | collective-permute-start | bytes 2359304 | tf_op jit(solution)/shard_map/ppermute | solution.py:21
  72.1 7.0 %collective-permute-start.5 = (bf16[64,864]{1,0:T(8,128)(2,1)S(1)}, bf16[64,864]{1,0:T(8,128)(2,1)S(1)}, u32[]{:S(2)}, u32[]{:S(2)}) collective-permute-start(bf16[64,864]{1,0:T(8,128)(2,1)S(1)} %get-tuple-element.15), channel_id=1, source_target_pairs={{0,0},{1,4},{2,8},{3,12},{4,1},{5,5},{6,9},{7,13},{8,2},{9,6},{10,... | collective-permute-start | bytes 331784 | tf_op jit(solution)/shard_map/ppermute | solution.py:440
  74.6 4.5 %collective-permute-start.6 = (bf16[64,864]{1,0:T(8,128)(2,1)S(1)}, bf16[64,864]{1,0:T(8,128)(2,1)S(1)}, u32[]{:S(2)}, u32[]{:S(2)}) collective-permute-start(bf16[64,864]{1,0:T(8,128)(2,1)S(1)} %get-tuple-element.16), channel_id=1, source_target_pairs={{0,1},{1,5},{2,9},{3,13},{4,2},{5,6},{6,10},{7,14},{8,3},{9,7},{10... | collective-permute-start | bytes 331784 | tf_op jit(solution)/shard_map/ppermute | solution.py:440
  74.6 11.4 %collective-permute-start.7 = (bf16[64,864]{1,0:T(8,128)(2,1)S(1)}, bf16[64,864]{1,0:T(8,128)(2,1)S(1)}, u32[]{:S(2)}, u32[]{:S(2)}) collective-permute-start(bf16[64,864]{1,0:T(8,128)(2,1)S(1)} %get-tuple-element.17), channel_id=1, source_target_pairs={{0,2},{1,6},{2,10},{3,14},{4,3},{5,7},{6,11},{7,15},{8,0},{9,4},{1... | collective-permute-start | bytes 331784 | tf_op jit(solution)/shard_map/ppermute | solution.py:440
  76.0 20.3 %collective-permute-start.8 = (bf16[64,864]{1,0:T(8,128)(2,1)S(1)}, bf16[64,864]{1,0:T(8,128)(2,1)S(1)}, u32[]{:S(2)}, u32[]{:S(2)}) collective-permute-start(bf16[64,864]{1,0:T(8,128)(2,1)S(1)} %get-tuple-element.18), channel_id=1, source_target_pairs={{0,3},{1,7},{2,11},{3,15},{4,0},{5,4},{6,8},{7,12},{8,1},{9,5},{10... | collective-permute-start | bytes 331784 | tf_op jit(solution)/shard_map/ppermute | solution.py:440
where the time goes:
time: 98.7 us; the launch traced here: 98.4 us
  waiting for transfers between devices  41.7 us (42%)
  Pallas kernels  30.8 us (31%)
  starting transfers between devices  13 us (13%)
  local copies, waits for them, and re-layouts  9.26 us (9%)
  other arithmetic  3.34 us (3%)
    ppermute x5, waiting for transfers between devices, from_behind(): lax.ppermute(array, axis, [(i, (i + by) % peers) for i in range(peers)])  24.5 us
    pallas_call x1, Pallas kernels, shards_kernels(): pl.pallas_call(functools.partial(smear_kernel, planes, rows), out_shape=j...  17.7 us
    ppermute x4, waiting for transfers between devices, shards_kernels(): lax.ppermute(blocks[k], ('brick', 'vec', 'sub'), pairs).astype(jnp.float32)  17.2 us
    pallas_call x1, Pallas kernels, shards_kernels(): pl.pallas_call(functools.partial(product_kernel, groups, rows, count, sca...  13.1 us
    ppermute x4, starting transfers between devices, shards_kernels(): lax.ppermute(blocks[k], ('brick', 'vec', 'sub'), pairs).astype(jnp.float32)  6.94 us
    ppermute x5, starting transfers between devices, from_behind(): lax.ppermute(array, axis, [(i, (i + by) % peers) for i in range(peers)])  6.09 us
    reshape x2, local copies, waits for them, and re-layouts, shards_kernels(): vectors.reshape((rows, 3, 2, planes, plane))  3.71 us
  transfers between devices with their start and end apart: 9, of which 6 were waited for; matrix products, arithmetic and copies ran while one was open for 5% of the time, Pallas kernels for 18%

commit v1 on v0

v1 whole, which is shorter than its diff:
```python
import functools
import math

import jax
import jax.numpy as jnp
from jax import lax
from jax.experimental import pallas as pl
from jax.experimental.pallas import tpu as pltpu
from jax.sharding import PartitionSpec as P

LY = 64
LZ = 8
ITERS = 2


KAPPA = 0.125


def from_behind(array, axis, by):
    peers = lax.axis_size(axis)
    return lax.ppermute(array, axis, [(i, (i + by) % peers) for i in range(peers)])


def padded_2(array, sides, width):
    for axis, dim in sides:
        peers, length = (lax.axis_size(axis), array.shape[dim])
        up = [(i, (i + 1) % peers) for i in range(peers)]
        down = [(j, i) for i, j in up]
        last = lax.slice_in_dim(array, length - width, length, axis=dim)
        initial = lax.slice_in_dim(array, 0, width, axis=dim)
        before = lax.ppermute(last, axis, up)
        after = lax.ppermute(initial, axis, down)
        array = jnp.concatenate([before, array, after], axis=dim)
    return array


def matrix_apply(matrix, source):
    matrix_real = matrix[:, :, 0][None]
    matrix_imag = matrix[:, :, 1][None]
    source_real = source[:, None, :, 0]
    source_imag = source[:, None, :, 1]
    real_part = jnp.sum(matrix_real * source_real - matrix_imag * source_imag, axis=2)
    imag_part = jnp.sum(matrix_real * source_imag + matrix_imag * source_real, axis=2)
    return jnp.stack([real_part, imag_part], axis=2)


def adjoint(matrix):
    return jnp.stack(
        [jnp.swapaxes(matrix[:, :, 0], 0, 1), -jnp.swapaxes(matrix[:, :, 1], 0, 1)], axis=2
    )


def step_depth(values, offset):
    depth_index = lax.iota(jnp.int32, values.shape[-1]) % LZ
    if offset > 0:
        return jnp.where(
            depth_index == LZ - 1, jnp.roll(values, LZ - 1, -1), jnp.roll(values, -1, -1)
        )
    return jnp.where(depth_index == 0, jnp.roll(values, 1 - LZ, -1), jnp.roll(values, 1, -1))


def step_column(values, offset):
    plane = LY * LZ
    column_index = lax.iota(jnp.int32, values.shape[-1]) // LZ % LY
    if offset > 0:
        return jnp.where(
            column_index == LY - 1, jnp.roll(values, plane - LZ, -1), jnp.roll(values, -LZ, -1)
        )
    return jnp.where(column_index == 0, jnp.roll(values, LZ - plane, -1), jnp.roll(values, LZ, -1))


def laplace_step(center, ahead, behind, here_links, back_links):
    forward = matrix_apply(here_links[0], ahead)
    backward = matrix_apply(adjoint(back_links), behind)
    total = forward + backward
    for direction, stepper in ((1, step_column), (2, step_depth)):
        forward = matrix_apply(here_links[direction], stepper(center, 1))
        backward = matrix_apply(adjoint(stepper(here_links[direction], -1)), stepper(center, -1))
        total = total + (forward + backward)
    return center + KAPPA * (total - 6.0 * center)


def shards(vectors, gauge_links, momenta):
    plane = LY * LZ
    local_sites = vectors.shape[3]
    raw_low = vectors.astype(jnp.bfloat16)
    field = vectors
    x_links = gauge_links[0]
    rim = from_behind(x_links[..., local_sites - plane :], "brick", 1)
    back_links = jnp.concatenate([rim, x_links[..., : local_sites - plane]], axis=3)
    for step in range(ITERS):
        padded = padded_2(field, (("brick", 3),), plane)
        field = laplace_step(
            padded[..., plane : plane + local_sites],
            padded[..., 2 * plane :],
            padded[..., :local_sites],
            gauge_links,
            back_links,
        )
    smeared_low = field.astype(jnp.bfloat16)
    raw_sites, smeared_sites = (
        lax.all_to_all(raw_low, ("vec", "sub"), split_axis=3, concat_axis=0, tiled=True),
        lax.all_to_all(smeared_low, ("vec", "sub"), split_axis=3, concat_axis=0, tiled=True),
    )
    groups = lax.axis_size(("vec", "sub"))
    total_vec = raw_sites.shape[0]
    width = raw_sites.shape[3]
    total_x = lax.axis_size("brick") * (local_sites // plane)
    first_site = lax.axis_index("brick") * local_sites + lax.axis_index(("vec", "sub")) * width
    site = first_site + lax.iota(jnp.int32, width)
    layer_index = (site // plane)[None]
    column_index = (site // LZ % LY)[None]
    depth_index = (site % LZ)[None]
    fraction = (
        jnp.mod(momenta[:, 0:1] * layer_index, total_x).astype(jnp.float32) / total_x
        + jnp.mod(momenta[:, 1:2] * column_index, LY).astype(jnp.float32) / LY
        + jnp.mod(momenta[:, 2:3] * depth_index, LZ).astype(jnp.float32) / LZ
    )
    angle = 2.0 * math.pi * fraction
    cosines = jnp.cos(angle)
    sines = jnp.sin(angle)
    right = smeared_sites.reshape((total_vec, 6 * width))
    scale = (3.0 * total_x * plane) ** (-0.5)

    def one_momentum(angles):
        cosine, sine = angles
        real_part = raw_sites[:, :, 0] * cosine - raw_sites[:, :, 1] * sine
        imag_part = raw_sites[:, :, 0] * sine + raw_sites[:, :, 1] * cosine
        phased = jnp.stack([real_part, imag_part], axis=2).astype(jnp.bfloat16)
        turned = jnp.stack([-phased[:, :, 1], phased[:, :, 0]], axis=2)
        left = jnp.concatenate(
            [
                phased.reshape((lax.axis_size(("vec", "sub")) * (total_vec // groups), 6 * width)),
                turned.reshape((lax.axis_size(("vec", "sub")) * (total_vec // groups), 6 * width)),
            ],
            axis=0,
        )
        product = lax.dot_general(
            left, right, (((1,), (1,)), ((), ())), preferred_element_type=jnp.float32
        )
        return product.reshape(
            (2, lax.axis_size(("vec", "sub")) * (total_vec // groups), total_vec)
        )

    blocks = lax.map(one_momentum, (cosines, sines))
    shares = lax.psum_scatter(
        jnp.transpose(blocks, (2, 0, 1, 3)) * scale, ("vec", "sub"), scatter_dimension=0, tiled=True
    )
    return lax.psum_scatter(shares, "brick", scatter_dimension=3, tiled=True)


def fused_kernel(plan, mom_ref, v_ref, g_ref, out_ref, *scratch):
    (vst, gst, field, table, moved, right, smeared, left0, left1, cosb, sinb, total, obuf, relay,
     rx, halo, hsend, lsend, lrecv, load_sem, halo_sem, link_sem, raw_sem, out_sem, last_sem) = scratch
    planes, rows, count, bricks, per, blocks_q, scale = plan
    plane = LY * LZ
    tiles = plane // 128
    all_tiles = planes * tiles
    f32, low = jnp.float32, jnp.bfloat16
    wide = 2 * plane
    last = planes - 1
    inner = list(range(1, last))
    outer = [0, last]
    position = {t: i for i, t in enumerate(inner + outer)}
    cut = len(inner) * 3 * wide
    span = planes * 3 * wide
    blocks = rows // 8
    half_blocks = blocks // 2
    trips = half_blocks * tiles
    b, v, s = (lax.axis_index(a) for a in ("brick", "vec", "sub"))
    left = (left0, left1)

    def remote(src, dst, sems, **ids):
        return pltpu.make_async_remote_copy(
            src_ref=src, dst_ref=dst, send_sem=sems.at[0], recv_sem=sems.at[1],
            device_id=ids, device_id_type=pl.DeviceIdType.MESH,
        )

    loads = {}
    for t in outer + inner:
        loads[t] = pltpu.make_async_copy(v_ref.at[:, t], vst.at[t], load_sem.at[t])
        loads[t].start()
    load_links = pltpu.make_async_copy(g_ref, gst.at[pl.ds(0, 54 * all_tiles)], load_sem.at[planes])
    load_links.start()
    barrier = pltpu.get_barrier_semaphore()
    for db in range(bricks):
        for ds in range(2):
            if db or ds:
                pl.semaphore_signal(
                    barrier, inc=1, device_id={"brick": (b + db) % bricks, "sub": (s + ds) % 2},
                    device_id_type=pl.DeviceIdType.MESH,
                )
    pl.semaphore_signal(
        barrier, inc=1, device_id={"vec": 1 - v}, device_id_type=pl.DeviceIdType.MESH
    )

    def unpack(t):
        flat = vst.at[t].reshape(rows * 3 * tiles * 2, 128)
        step = 3 * tiles * 2
        for c in range(3):
            for first in range(0, rows, 16):
                for part in range(2):
                    for lane in range(tiles):
                        start = first * step + c * tiles * 2 + lane * 2 + part
                        at = part * plane + lane * 128
                        pair = [flat[pl.ds(start + h * 8 * step, 8, stride=step), :] for h in range(2)]
                        for h in range(2):
                            field[0, t + 1, c, first + 8 * h : first + 8 * h + 8, at : at + 128] = pair[h]
                        k = (position[t] * 3 + c) * wide + at
                        right[first : first + 16, k : k + 128] = jnp.concatenate(pair, axis=0).astype(low)

    def link_rows(t, part, group):
        return jnp.concatenate(
            [
                gst[pl.ds(group * 16 * all_tiles + (t * tiles + lane) * 2 + part, 8, stride=2 * all_tiles), :]
                for lane in range(tiles)
            ],
            axis=1,
        ) * KAPPA

    for t in outer:
        loads[t].wait()
        unpack(t)
    load_links.wait()
    for part in range(2):
        both = jnp.concatenate([link_rows(last, part, 0), link_rows(last, part, 1)], axis=0)
        lsend[16 * part : 16 * part + 16, :] = both.astype(low)
    pl.semaphore_wait(barrier, 2 * bricks)
    up, down = (b + 1) % bricks, (b + bricks - 1) % bricks

    def halos(step, low_src, high_src):
        return (
            remote(high_src, halo.at[step, 0], halo_sem.at[step, 0], brick=up),
            remote(low_src, halo.at[step, 1], halo_sem.at[step, 1], brick=down),
        )

    def own(t):
        return right.at[0:rows, position[t] * 3 * wide : (position[t] + 1) * 3 * wide]

    first_halos = halos(0, own(0), own(last))
    links_up = remote(lsend, lrecv, link_sem, brick=up)
    links_up.start()
    for copy in first_halos:
        copy.start()
    for t in inner:
        loads[t].wait()
        unpack(t)
    parts = (slice(0, cut), slice(cut, span))
    unit = 2 * rows

    def raw_copy(index, from_slot, to_slot, ks, **ids):
        return remote(
            right.at[from_slot * unit : from_slot * unit + rows, ks],
            right.at[to_slot * unit : to_slot * unit + rows, ks],
            raw_sem.at[index], **ids,
        )

    across = [raw_copy(i, 0, 2, parts[i], vec=1 - v) for i in range(2)]
    beside = raw_copy(2, 0, 1, slice(0, span), sub=1 - s)
    onward = [raw_copy(3 + i, 2, 3, parts[i], sub=1 - s) for i in range(2)]
    for copy in across + [beside]:
        copy.start()

    depth_wide = lax.broadcasted_iota(jnp.int32, (8, plane), 1) % LZ
    depth = lax.broadcasted_iota(jnp.int32, (8, 128), 1) % LZ

    def spread(t, carry):
        for part in range(2):
            for group in range(4):
                here = link_rows(t, part, group)
                if group > 0:
                    by = pltpu.roll(here, LZ, 1)
                    bz = jnp.where(
                        depth_wide == 0, pltpu.roll(here, plane - (LZ - 1), 1), pltpu.roll(here, 1, 1)
                    )
                for j in range(min(8, 27 - 8 * group)):
                    index = group * 8 + j
                    row = jnp.broadcast_to(here[j : j + 1], (8, plane))
                    table[t, index * 2 + part] = row
                    if index < 9:
                        table[t + 1, 54 + index * 2 + part] = row
                    else:
                        back = by if index < 18 else bz
                        table[t, 54 + index * 2 + part] = jnp.broadcast_to(back[j : j + 1], (8, plane))
        return carry

    lax.fori_loop(0, planes, spread, 0)

    def phases(q, carry):
        n = [mom_ref[d, jnp.minimum(q, count - 1)].astype(f32) for d in range(3)]
        for group in range(0, all_tiles, 8):
            height = min(8, all_tiles - group)
            site = (
                lax.broadcasted_iota(jnp.int32, (height, 128), 0) * 128
                + lax.broadcasted_iota(jnp.int32, (height, 128), 1)
                + group * 128
            )
            x = (site // plane + b * planes).astype(f32)
            y = (site // LZ % LY).astype(f32)
            z = (site % LZ).astype(f32)
            turns = n[0] * x / (bricks * planes) + n[1] * y / LY + n[2] * z / LZ
            angle = (2.0 * math.pi) * (turns - jnp.round(turns))
            cosine, sine = jnp.cos(angle), jnp.sin(angle)
            for j in range(height):
                at = (group + j) * 128
                cosb[q, :, at : at + 128] = jnp.broadcast_to(cosine[j : j + 1], (16, 128)).astype(low)
                sinb[q, :, at : at + 128] = jnp.broadcast_to(sine[j : j + 1], (16, 128)).astype(low)
        return carry

    lax.fori_loop(0, per * blocks_q, phases, 0)

    def shift(stage, k, to):
        step, t = stage
        rows_at = pl.ds(pl.multiple_of(k % blocks * 8, 8), 8)
        first_lane = k // blocks * plane
        lanes = pl.ds(pl.multiple_of(first_lane, plane), plane)
        for c in range(3):
            w = field[step, t + 1, c, rows_at, lanes]
            moved[to, 0, c, rows_at, lanes] = pltpu.roll(w, plane - LZ, 1)
            moved[to, 1, c, rows_at, lanes] = pltpu.roll(w, LZ, 1)
            for part in range(tiles):
                u = w[:, part * 128 : part * 128 + 128]
                here = pl.ds(pl.multiple_of(first_lane + part * 128, 128), 128)
                moved[to, 2, c, rows_at, here] = jnp.where(
                    depth == LZ - 1, pltpu.roll(u, LZ - 1, 1), pltpu.roll(u, 127, 1)
                )
                moved[to, 3, c, rows_at, here] = jnp.where(
                    depth == 0, pltpu.roll(u, 128 - (LZ - 1), 1), pltpu.roll(u, 1, 1)
                )

    def block(stage, k, at_moved):
        step, t = stage
        lane, first = k // half_blocks, k % half_blocks * 16
        lanes = (
            pl.ds(pl.multiple_of(lane * 128, 128), 128),
            pl.ds(pl.multiple_of(plane + lane * 128, 128), 128),
        )
        at_rows = [pl.ds(pl.multiple_of(first + 8 * h, 8), 8) for h in range(2)]
        acc = {}
        for h in range(2):
            for r in range(3):
                for part in range(2):
                    mid = field[step, t + 1, r, at_rows[h], lanes[part]]
                    acc[h, r, part] = (1.0 - 6.0 * KAPPA) * mid
        for way in range(6):
            direction, back = way // 2, way % 2
            for c in range(3):
                sources = []
                for h in range(2):
                    if direction == 0:
                        p = t + 2 - 2 * back
                        sources.append([field[step, p, c, at_rows[h], lanes[i]] for i in range(2)])
                    else:
                        sources.append([moved[at_moved, way - 2, c, at_rows[h], lanes[i]] for i in range(2)])
                for r in range(3):
                    row = direction * 18 + (54 + c * 6 + r * 2 if back else r * 6 + c * 2)
                    ur = table[t, row, :, lanes[0]]
                    ui = table[t, row + 1, :, lanes[0]]
                    for h, (sr, si) in enumerate(sources):
                        if back:
                            acc[h, r, 0] = acc[h, r, 0] + (ur * sr + ui * si)
                            acc[h, r, 1] = acc[h, r, 1] + (ur * si - ui * sr)
                        else:
                            acc[h, r, 0] = acc[h, r, 0] + (ur * sr - ui * si)
                            acc[h, r, 1] = acc[h, r, 1] + (ur * si + ui * sr)
        both = pl.ds(pl.multiple_of(first, 16), 16)
        for r in range(3):
            for part in range(2):
                if step == 0:
                    for h in range(2):
                        field[1, t + 1, r, at_rows[h], lanes[part]] = acc[h, r, part]
                if step == 1 or t in outer:
                    pair = jnp.concatenate([acc[0, r, part], acc[1, r, part]], axis=0).astype(low)
                    if step == 1:
                        smeared[position[t] * 3 + r, both, lanes[part]] = pair
                    else:
                        k_at = pl.ds(pl.multiple_of((2 * r + part) * plane + lane * 128, 128), 128)
                        hsend[outer.index(t), both, k_at] = pair

    stages = [(step, t) for step in range(2) for t in inner + outer]

    def run(i):
        def trip(k, carry):
            if i + 1 < len(stages):
                shift(stages[i + 1], k, (i + 1) % 2)
            block(stages[i], k, i % 2)
            return carry

        lax.fori_loop(0, trips, trip, 0)

    def begin(k, carry):
        shift(stages[0], k, 0)
        return carry

    lax.fori_loop(0, trips, begin, 0)
    for i in range(len(inner)):
        run(i)

    def take(step, side):
        to = planes + 1 if side else 0
        for c in range(3):
            field[step, to, c] = halo[step, side, :, c * wide : (c + 1) * wide].astype(f32)

    links_up.wait_recv()
    for part in range(2):
        got = lrecv[16 * part : 16 * part + 16, :].astype(f32)
        for index in range(9):
            table[0, 54 + index * 2 + part] = jnp.broadcast_to(got[index : index + 1], (8, plane))
    at = len(inner)
    second_halos = halos(1, hsend.at[0], hsend.at[1])
    for side in range(2):
        first_halos[side].wait_recv()
        take(0, side)
        run(at + side)
        second_halos[1 - side].start()
    across[0].wait_recv()
    onward[0].start()
    for i in range(len(inner)):
        run(at + 2 + i)
    beside.wait_recv()
    onward[0].wait_recv()

    def fill(k, carry):
        re = pl.ds(pl.multiple_of(k * wide, wide), plane)
        im = pl.ds(pl.multiple_of(k * wide + plane, plane), plane)
        for slot in range(4):
            at_raw = slice(slot * unit, slot * unit + rows)
            at_turned = slice(slot * unit + rows, (slot + 1) * unit)
            right[at_turned, re] = -right[at_raw, im]
            right[at_turned, im] = right[at_raw, re]
        return carry

    def turn(half, qb, to):
        for j in range(per):
            q = qb * per + j
            for i, t in enumerate(half):
                for lane in range(0, plane, 128):
                    cosine = cosb[q, :, t * plane + lane : t * plane + lane + 128]
                    sine = sinb[q, :, t * plane + lane : t * plane + lane + 128]
                    for c in range(3):
                        for row in range(0, rows, 16):
                            k = position[t] * 3 + c
                            sr = smeared[k, row : row + 16, lane : lane + 128]
                            si = smeared[k, row : row + 16, plane + lane : plane + lane + 128]
                            at_rows = slice(j * rows + row, j * rows + row + 16)
                            col = (i * 3 + c) * wide + lane
                            to[at_rows, col : col + 128] = cosine * sr + sine * si
                            to[at_rows, col + plane : col + plane + 128] = cosine * si - sine * sr

    def product(half, qb, following, side, finish):
        ks = parts[0] if half is inner else parts[1]
        part = lax.dot_general(
            right[:, ks], left[side][:, 0 : ks.stop - ks.start], (((1,), (1,)), ((), ())),
            preferred_element_type=f32,
        )
        turn(half, following, left[1 - side])
        finish(qb, part)

    def products(half, finish):
        turn(half, 0, left[0])

        def two(h, carry):
            product(half, 2 * h, 2 * h + 1, 0, finish)
            product(half, 2 * h + 1, jnp.minimum(2 * h + 2, blocks_q - 1), 1, finish)
            return carry

        lax.fori_loop(0, blocks_q // 2, two, 0)

    def keep(qb, part):
        total[qb] = part

    lax.fori_loop(0, len(inner) * 3, fill, 0)
    products(inner, keep)
    across[1].wait_recv()
    onward[1].start()
    for side in range(2):
        second_halos[side].wait_recv()
        take(1, side)
        run(at + len(inner) + 2 + side)
    onward[1].wait_recv()
    lax.fori_loop(len(inner) * 3, planes * 3, fill, 0)

    def cross(qb):
        return remote(obuf.at[qb, 2 * unit : 4 * unit], relay.at[qb], out_sem.at[qb], vec=1 - v)

    def along(qb, hop, ds):
        root = (v if hop == 0 else 1 - v) * 2 + s
        source = obuf if hop == 0 else relay
        src = source.at[qb, ds * unit : (ds + 1) * unit]
        dst = rx.at[qb, b]
        sems = last_sem.at[qb]
        far = pltpu.make_async_remote_copy(
            src_ref=src, dst_ref=dst, send_sem=sems.at[bricks + hop * 2 + ds], recv_sem=sems.at[b],
            device_id={"brick": root, "sub": (s + ds) % 2}, device_id_type=pl.DeviceIdType.MESH,
        )
        near = pltpu.make_async_copy(src, dst, sems.at[b])
        return root, far, near

    def depart(qb, hop):
        for ds in range(2):
            root, far, near = along(qb, hop, ds)
            if ds:
                far.start()
            else:
                pl.when(root == b)(near.start)
                pl.when(root != b)(far.start)

    def hand_on(qb):
        cross(qb).wait_recv()
        depart(qb, 1)

    def ship(qb, part):
        obuf[qb] = ((total[qb] + part) * scale).astype(low)
        cross(qb).start()
        depart(qb, 0)
        pl.when(qb > 0)(lambda: hand_on(qb - 1))

    products(outer, ship)
    hand_on(blocks_q - 1)
    for qb in range(blocks_q):
        acc = None
        for i in range(bricks):
            pltpu.make_async_copy(rx.at[qb, i], rx.at[qb, i], last_sem.at[qb, i]).wait()
            got = rx[qb, i].astype(f32)
            acc = got if acc is None else acc + got
        out_ref[:, qb * per * rows : (qb + 1) * per * rows] = acc
    for copy in (links_up, *first_halos, *second_halos, *across, beside, *onward):
        copy.wait_send()
    for qb in range(blocks_q):
        cross(qb).wait_send()
        for hop in range(2):
            for ds in range(2):
                root, far, near = along(qb, hop, ds)
                if ds:
                    far.wait_send()
                else:
                    pl.when(root != b)(far.wait_send)


def shards_fused(vectors, gauge_links, momenta):
    plane = LY * LZ
    rows, local_sites = vectors.shape[0], vectors.shape[3]
    planes = local_sites // plane
    tiles = plane // 128
    bricks = lax.axis_size("brick")
    count = momenta.shape[0]
    per = 256 // rows
    blocks_q = 2 * (-(-count // (2 * per)))
    low, f32 = jnp.bfloat16, jnp.float32
    v = vectors.reshape((rows, 3, 2, planes * tiles, 128)).transpose((0, 1, 3, 2, 4))
    v = v.reshape((rows * 3, planes, tiles * 2, 128))
    g = gauge_links.reshape((27, 2, planes * tiles, 128)).transpose((0, 2, 1, 3))
    g = g.reshape((54 * planes * tiles, 128))
    wide = 2 * plane
    most = max(2, planes - 2) * 3 * wide
    scale = (3.0 * bricks * local_sites) ** (-0.5)
    vmem, dma = pltpu.VMEM, pltpu.SemaphoreType.DMA
    plan = (planes, rows, count, bricks, per, blocks_q, scale)
    out = pl.pallas_call(
        functools.partial(fused_kernel, plan),
        out_shape=jax.ShapeDtypeStruct((2 * rows, blocks_q * per * rows), f32),
        in_specs=[
            pl.BlockSpec(memory_space=pltpu.SMEM),
            pl.BlockSpec(memory_space=pl.ANY),
            pl.BlockSpec(memory_space=pl.ANY),
        ],
        out_specs=pl.BlockSpec(memory_space=pltpu.VMEM),
        scratch_shapes=[
            vmem((planes, rows * 3, tiles * 2, 128), f32),
            vmem((64 * planes * tiles, 128), f32),
            vmem((2, planes + 2, 3, rows, wide), f32),
            vmem((planes + 1, 108, 8, plane), f32),
            vmem((2, 4, 3, rows, wide), f32),
            vmem((8 * rows, planes * 3 * wide), low),
            vmem((planes * 3, rows, wide), low),
            vmem((per * rows, most), low),
            vmem((per * rows, most), low),
            vmem((per * blocks_q, 16, local_sites), low),
            vmem((per * blocks_q, 16, local_sites), low),
            vmem((blocks_q, 8 * rows, per * rows), f32),
            vmem((blocks_q, 8 * rows, per * rows), low),
            vmem((blocks_q, 4 * rows, per * rows), low),
            vmem((blocks_q, bricks, 2 * rows, per * rows), low),
            vmem((2, 2, rows, 3 * wide), low),
            vmem((2, rows, 3 * wide), low),
            vmem((32, plane), low),
            vmem((32, plane), low),
            dma((planes + 1,)),
            dma((2, 2, 2)),
            dma((2,)),
            dma((5, 2)),
            dma((blocks_q, 2)),
            dma((blocks_q, bricks + 4)),
        ],
        compiler_params=pltpu.CompilerParams(
            vmem_limit_bytes=60 * 2**20, collective_id=0, has_side_effects=True
        ),
        name="elementals",
    )(momenta.T, v, g)
    out = out.reshape((2, rows, blocks_q * per, rows))[:, :, :count]
    return jnp.transpose(out, (1, 2, 0, 3))


def choose(vectors, gauge_links, momenta):
    plane = LY * LZ
    bricks, vecs, subs = (lax.axis_size(a) for a in ("brick", "vec", "sub"))
    rows, local_sites = vectors.shape[0], vectors.shape[3]
    fits = local_sites % plane == 0 and 3 <= local_sites // plane <= 4 and rows == 32
    if fits and vecs == 2 and subs == 2 and bricks == 4:
        return shards_fused(vectors, gauge_links, momenta)
    return shards(vectors, gauge_links, momenta)


def solution(mesh):
    in_specs = (
        P(("vec", "sub"), None, None, ("grp", "brick")),
        P(None, None, None, None, ("grp", "brick")),
        P(),
    )
    out_specs = P(("vec", "sub"), "grp", None, "brick")
    return jax.shard_map(choose, mesh=mesh, in_specs=in_specs, out_specs=out_specs, check_vma=False)
```

time: 98.7 us -> 55 us (0.56)
  the two profiles are of different devices: /device:TPU:1 before, /device:TPU:2 now
where the time goes in v1:
time: 55 us; the launch traced here: 54.5 us
  Pallas kernels  51.6 us (94%)
  local copies, waits for them, and re-layouts  2.9 us (5%)
    pallas_call x1, Pallas kernels, shards_fused(): pl.pallas_call(functools.partial(fused_kernel, plan), out_shape=jax.Shape...  51.6 us
    unnamed x1, local copies, waits for them, and re-layouts  1.61 us
    reshape x1, local copies, waits for them, and re-layouts, shards_fused(): out = out.reshape((2, rows, blocks_q * per, rows))[:, :, :count]  1.29 us

profile of v1, /device:TPU:2, one launch (start us, length us, event | category | flops | bytes accessed | tf_op | source)
XLA Modules:
  0.0 54.5 jit_solution(6767600819676346114)
XLA Ops:
  0.0 51.6 %elementals.1 = f32[64,1024]{1,0:T(8,128)} custom-call(s32[3,27]{1,0:T(4,128)} %bitcast.18, f32[96,4,8,128]{3,2,1,0:T(8,128)} %bitcast.16, f32[864,128]{1,0:T(8,128)} %bitcast.17), custom_call_target="tpu_custom_call" | custom-call | tf_op jit(solution)/shard_map/elementals/pallas_call | solution.py:559
  51.6 1.3 %reshape.19 = f32[2,32,32,32]{3,2,1,0:T(8,128)S(1)} reshape(f32[64,1024]{1,0:T(8,128)} %elementals.1) | data formatting | bytes 524288 | tf_op jit(solution)/shard_map/reshape | solution.py:600
  52.9 1.6 %copy.9 = f32[2,32,27,32]{3,0,2,1:T(2,128)} copy(f32[2,32,27,32]{3,2,1,0:T(8,128)S(1)} %bitcast.15) | data formatting | bytes 442368

commit v2 on v1

--- a/solution.py
+++ b/solution.py
@@ -150,9 +150,11 @@
 
 
 def fused_kernel(plan, mom_ref, v_ref, g_ref, out_ref, *scratch):
-    (vst, gst, field, table, moved, right, smeared, left0, left1, cosb, sinb, total, obuf, relay,
-     rx, halo, hsend, lsend, lrecv, load_sem, halo_sem, link_sem, raw_sem, out_sem, last_sem) = scratch
+    (vst, gst, field0, field1, table, moved0, moved1, right, smeared, left0, left1, cosb, sinb, total, obuf,
+     relay, rx, halo, hsend, lsend, lrecv, load_sem, halo_sem, link_sem, raw_sem, out_sem, last_sem) = scratch
     planes, rows, count, bricks, per, blocks_q, scale = plan
+    fields, moved = (field0, field1), (moved0, moved1)
+    halves = rows // 16
     plane = LY * LZ
     tiles = plane // 128
     all_tiles = planes * tiles
@@ -164,9 +166,6 @@
     position = {t: i for i, t in enumerate(inner + outer)}
     cut = len(inner) * 3 * wide
     span = planes * 3 * wide
-    blocks = rows // 8
-    half_blocks = blocks // 2
-    trips = half_blocks * tiles
     b, v, s = (lax.axis_index(a) for a in ("brick", "vec", "sub"))
     left = (left0, left1)
 
@@ -200,14 +199,19 @@
         for c in range(3):
             for first in range(0, rows, 16):
                 for part in range(2):
-                    for lane in range(tiles):
-                        start = first * step + c * tiles * 2 + lane * 2 + part
+                    for lane in range(0, tiles, 2):
                         at = part * plane + lane * 128
-                        pair = [flat[pl.ds(start + h * 8 * step, 8, stride=step), :] for h in range(2)]
+                        quad = []
                         for h in range(2):
-                            field[0, t + 1, c, first + 8 * h : first + 8 * h + 8, at : at + 128] = pair[h]
+                            start = (first + 8 * h) * step + c * tiles * 2 + lane * 2 + part
+                            quad.append(
+                                jnp.concatenate(
+                                    [flat[pl.ds(start + 2 * i, 8, stride=step), :] for i in range(2)], axis=1
+                                )
+                            )
+                            field0[t + 1, c, first + 8 * h : first + 8 * h + 8, at : at + 256] = quad[h]
                         k = (position[t] * 3 + c) * wide + at
-                        right[first : first + 16, k : k + 128] = jnp.concatenate(pair, axis=0).astype(low)
+                        right[first : first + 16, k : k + 256] = jnp.concatenate(quad, axis=0).astype(low)
 
     def link_rows(t, part, group):
         return jnp.concatenate(
@@ -228,20 +232,26 @@
     pl.semaphore_wait(barrier, 2 * bricks)
     up, down = (b + 1) % bricks, (b + bricks - 1) % bricks
 
-    def halos(step, low_src, high_src):
+    def halos(step, h, low_src, high_src):
+        sems = halo_sem.at[step, h]
         return (
-            remote(high_src, halo.at[step, 0], halo_sem.at[step, 0], brick=up),
-            remote(low_src, halo.at[step, 1], halo_sem.at[step, 1], brick=down),
-        )
-
-    def own(t):
-        return right.at[0:rows, position[t] * 3 * wide : (position[t] + 1) * 3 * wide]
-
-    first_halos = halos(0, own(0), own(last))
+            remote(high_src, halo.at[step, h, 0], sems.at[0], brick=up),
+            remote(low_src, halo.at[step, h, 1], sems.at[1], brick=down),
+        )
+
+    def own(t, h):
+        at = position[t] * 3 * wide
+        return right.at[16 * h : 16 * h + 16, at : at + 3 * wide]
+
+    copies = {}
     links_up = remote(lsend, lrecv, link_sem, brick=up)
-    links_up.start()
-    for copy in first_halos:
-        copy.start()
+    for h in range(halves):
+        copies[0, h] = halos(0, h, own(0, h), own(last, h))
+        copies[1, h] = halos(1, h, hsend.at[h, 0], hsend.at[h, 1])
+        for copy in copies[0, h]:
+            copy.start()
+        if h == 0:
+            links_up.start()
     for t in inner:
         loads[t].wait()
         unpack(t)
@@ -286,61 +296,78 @@
 
     lax.fori_loop(0, planes, spread, 0)
 
+    places = []
+    for group in range(0, all_tiles, 8):
+        height = min(8, all_tiles - group)
+        site = (
+            lax.broadcasted_iota(jnp.int32, (height, 128), 0) * 128
+            + lax.broadcasted_iota(jnp.int32, (height, 128), 1)
+            + group * 128
+        )
+        places.append(
+            (
+                (site // plane + b * planes).astype(f32) * (1.0 / (bricks * planes)),
+                (site // LZ % LY).astype(f32) * (1.0 / LY),
+                (site % LZ).astype(f32) * (1.0 / LZ),
+            )
+        )
+
     def phases(q, carry):
         n = [mom_ref[d, jnp.minimum(q, count - 1)].astype(f32) for d in range(3)]
-        for group in range(0, all_tiles, 8):
-            height = min(8, all_tiles - group)
-            site = (
-                lax.broadcasted_iota(jnp.int32, (height, 128), 0) * 128
-                + lax.broadcasted_iota(jnp.int32, (height, 128), 1)
-                + group * 128
-            )
-            x = (site // plane + b * planes).astype(f32)
-            y = (site // LZ % LY).astype(f32)
-            z = (site % LZ).astype(f32)
-            turns = n[0] * x / (bricks * planes) + n[1] * y / LY + n[2] * z / LZ
-            angle = (2.0 * math.pi) * (turns - jnp.round(turns))
-            cosine, sine = jnp.cos(angle), jnp.sin(angle)
-            for j in range(height):
-                at = (group + j) * 128
+        for group, (x, y, z) in enumerate(places):
+            turns = n[0] * x + n[1] * y + n[2] * z
+            half = jnp.round(2.0 * turns)
+            sign = 1.0 - 2.0 * jnp.abs(half - 2.0 * jnp.round(0.5 * half))
+            angle = (2.0 * math.pi) * (turns - 0.5 * half)
+            square = angle * angle
+            cosine, sine = 0.0, 0.0
+            for i in range(7, 0, -1):
+                cosine = (cosine * square) + (-1.0) ** i / math.factorial(2 * i)
+            cosine = sign * (1.0 + cosine * square)
+            for i in range(6, 0, -1):
+                sine = (sine * square) + (-1.0) ** i / math.factorial(2 * i + 1)
+            sine = sign * (angle + angle * (sine * square))
+            for j in range(x.shape[0]):
+                at = (group * 8 + j) * 128
                 cosb[q, :, at : at + 128] = jnp.broadcast_to(cosine[j : j + 1], (16, 128)).astype(low)
                 sinb[q, :, at : at + 128] = jnp.broadcast_to(sine[j : j + 1], (16, 128)).astype(low)
         return carry
 
-    lax.fori_loop(0, per * blocks_q, phases, 0)
+    lax.fori_loop(0, count, phases, 0)
 
     def shift(stage, k, to):
-        step, t = stage
-        rows_at = pl.ds(pl.multiple_of(k % blocks * 8, 8), 8)
-        first_lane = k // blocks * plane
+        step, t, h = stage
+        rows_to = pl.ds(pl.multiple_of(k % 2 * 8, 8), 8)
+        rows_at = pl.ds(pl.multiple_of(h * 16 + k % 2 * 8, 8), 8)
+        first_lane = k // 2 * plane
         lanes = pl.ds(pl.multiple_of(first_lane, plane), plane)
         for c in range(3):
-            w = field[step, t + 1, c, rows_at, lanes]
-            moved[to, 0, c, rows_at, lanes] = pltpu.roll(w, plane - LZ, 1)
-            moved[to, 1, c, rows_at, lanes] = pltpu.roll(w, LZ, 1)
+            w = fields[step][t + 1, c, rows_at, lanes]
+            to[0, c, rows_to, lanes] = pltpu.roll(w, plane - LZ, 1)
+            to[1, c, rows_to, lanes] = pltpu.roll(w, LZ, 1)
             for part in range(tiles):
                 u = w[:, part * 128 : part * 128 + 128]
                 here = pl.ds(pl.multiple_of(first_lane + part * 128, 128), 128)
-                moved[to, 2, c, rows_at, here] = jnp.where(
+                to[2, c, rows_to, here] = jnp.where(
                     depth == LZ - 1, pltpu.roll(u, LZ - 1, 1), pltpu.roll(u, 127, 1)
                 )
-                moved[to, 3, c, rows_at, here] = jnp.where(
+                to[3, c, rows_to, here] = jnp.where(
                     depth == 0, pltpu.roll(u, 128 - (LZ - 1), 1), pltpu.roll(u, 1, 1)
                 )
 
-    def block(stage, k, at_moved):
-        step, t = stage
-        lane, first = k // half_blocks, k % half_blocks * 16
+    def block(stage, lane, now):
+        step, t, half = stage
+        field = fields[step]
         lanes = (
             pl.ds(pl.multiple_of(lane * 128, 128), 128),
             pl.ds(pl.multiple_of(plane + lane * 128, 128), 128),
         )
-        at_rows = [pl.ds(pl.multiple_of(first + 8 * h, 8), 8) for h in range(2)]
+        at_rows = [slice(half * 16 + 8 * h, half * 16 + 8 * h + 8) for h in range(2)]
         acc = {}
         for h in range(2):
             for r in range(3):
                 for part in range(2):
-                    mid = field[step, t + 1, r, at_rows[h], lanes[part]]
+                    mid = field[t + 1, r, at_rows[h], lanes[part]]
                     acc[h, r, part] = (1.0 - 6.0 * KAPPA) * mid
         for way in range(6):
             direction, back = way // 2, way % 2
@@ -349,9 +376,9 @@
                 for h in range(2):
                     if direction == 0:
                         p = t + 2 - 2 * back
-                        sources.append([field[step, p, c, at_rows[h], lanes[i]] for i in range(2)])
+                        sources.append([field[p, c, at_rows[h], lanes[i]] for i in range(2)])
                     else:
-                        sources.append([moved[at_moved, way - 2, c, at_rows[h], lanes[i]] for i in range(2)])
+                        sources.append([now[way - 2, c, 8 * h : 8 * h + 8, lanes[i]] for i in range(2)])
                 for r in range(3):
                     row = direction * 18 + (54 + c * 6 + r * 2 if back else r * 6 + c * 2)
                     ur = table[t, row, :, lanes[0]]
@@ -363,60 +390,66 @@
                         else:
                             acc[h, r, 0] = acc[h, r, 0] + (ur * sr - ui * si)
                             acc[h, r, 1] = acc[h, r, 1] + (ur * si + ui * sr)
-        both = pl.ds(pl.multiple_of(first, 16), 16)
+        both = slice(half * 16, half * 16 + 16)
         for r in range(3):
             for part in range(2):
                 if step == 0:
                     for h in range(2):
-                        field[1, t + 1, r, at_rows[h], lanes[part]] = acc[h, r, part]
+                        field1[t + 1, r, at_rows[h], lanes[part]] = acc[h, r, part]
                 if step == 1 or t in outer:
                     pair = jnp.concatenate([acc[0, r, part], acc[1, r, part]], axis=0).astype(low)
                     if step == 1:
                         smeared[position[t] * 3 + r, both, lanes[part]] = pair
                     else:
                         k_at = pl.ds(pl.multiple_of((2 * r + part) * plane + lane * 128, 128), 128)
-                        hsend[outer.index(t), both, k_at] = pair
-
-    stages = [(step, t) for step in range(2) for t in inner + outer]
-
-    def run(i):
-        def trip(k, carry):
-            if i + 1 < len(stages):
-                shift(stages[i + 1], k, (i + 1) % 2)
-            block(stages[i], k, i % 2)
-            return carry
-
-        lax.fori_loop(0, trips, trip, 0)
+                        hsend[half, outer.index(t), :, k_at] = pair
+
+    stages = [(0, t, h) for h in range(halves) for t in inner]
+    for h in range(halves):
+        stages += [(0, t, h) for t in outer] + [(1, t, h) for t in inner]
+    stages += [(1, t, h) for h in range(halves) for t in outer]
+
+    def run(step, ts, h):
+        for t in ts:
+            i = stages.index((step, t, h))
+
+            def trip(k, carry):
+                if i + 1 < len(stages):
+                    shift(stages[i + 1], k, moved[(i + 1) % 2])
+                block(stages[i], k, moved[i % 2])
+                return carry
+
+            lax.fori_loop(0, tiles, trip, 0)
 
     def begin(k, carry):
-        shift(stages[0], k, 0)
+        shift(stages[0], k, moved[0])
         return carry
 
-    lax.fori_loop(0, trips, begin, 0)
-    for i in range(len(inner)):
-        run(i)
-
-    def take(step, side):
-        to = planes + 1 if side else 0
+    lax.fori_loop(0, tiles, begin, 0)
+    for h in range(halves):
+        run(0, inner, h)
+
+    def take(step, h, side):
+        copies[step, h][side].wait_recv()
         for c in range(3):
-            field[step, to, c] = halo[step, side, :, c * wide : (c + 1) * wide].astype(f32)
+            fields[step][planes + 1 if side else 0, c, 16 * h : 16 * h + 16] = (
+                halo[step, h, side, :, c * wide : (c + 1) * wide].astype(f32)
+            )
 
     links_up.wait_recv()
     for part in range(2):
         got = lrecv[16 * part : 16 * part + 16, :].astype(f32)
         for index in range(9):
             table[0, 54 + index * 2 + part] = jnp.broadcast_to(got[index : index + 1], (8, plane))
-    at = len(inner)
-    second_halos = halos(1, hsend.at[0], hsend.at[1])
-    for side in range(2):
-        first_halos[side].wait_recv()
-        take(0, side)
-        run(at + side)
-        second_halos[1 - side].start()
-    across[0].wait_recv()
-    onward[0].start()
-    for i in range(len(inner)):
-        run(at + 2 + i)
+    for h in range(halves):
+        for side in range(2):
+            take(0, h, side)
+            run(0, [outer[side]], h)
+            copies[1, h][1 - side].start()
+        if h == halves - 1:
+            across[0].wait_recv()
+            onward[0].start()
+        run(1, inner, h)
     beside.wait_recv()
     onward[0].wait_recv()
 
@@ -430,111 +463,134 @@
             right[at_turned, im] = right[at_raw, re]
         return carry
 
-    def turn(half, qb, to):
-        for j in range(per):
+    blocks = [(h, half, qb) for h in range(halves) for half in range(2) for qb in range(blocks_q)]
+    members = (inner, outer)
+
+    def turn(i):
+        h, half, qb = blocks[i]
+        to = left[i % 2]
+        for j in range(min(per, count - qb * per)):
             q = qb * per + j
-            for i, t in enumerate(half):
-                for lane in range(0, plane, 128):
-                    cosine = cosb[q, :, t * plane + lane : t * plane + lane + 128]
-                    sine = sinb[q, :, t * plane + lane : t * plane + lane + 128]
+            for n, t in enumerate(members[half]):
+                for lane in range(0, plane, 256):
+                    cosine = cosb[q, :, t * plane + lane : t * plane + lane + 256]
+                    sine = sinb[q, :, t * plane + lane : t * plane + lane + 256]
                     for c in range(3):
-                        for row in range(0, rows, 16):
-                            k = position[t] * 3 + c
-                            sr = smeared[k, row : row + 16, lane : lane + 128]
-                            si = smeared[k, row : row + 16, plane + lane : plane + lane + 128]
-                            at_rows = slice(j * rows + row, j * rows + row + 16)
-                            col = (i * 3 + c) * wide + lane
-                            to[at_rows, col : col + 128] = cosine * sr + sine * si
-                            to[at_rows, col + plane : col + plane + 128] = cosine * si - sine * sr
-
-    def product(half, qb, following, side, finish):
-        ks = parts[0] if half is inner else parts[1]
-        part = lax.dot_general(
-            right[:, ks], left[side][:, 0 : ks.stop - ks.start], (((1,), (1,)), ((), ())),
-            preferred_element_type=f32,
-        )
-        turn(half, following, left[1 - side])
-        finish(qb, part)
-
-    def products(half, finish):
-        turn(half, 0, left[0])
-
-        def two(h, carry):
-            product(half, 2 * h, 2 * h + 1, 0, finish)
-            product(half, 2 * h + 1, jnp.minimum(2 * h + 2, blocks_q - 1), 1, finish)
-            return carry
-
-        lax.fori_loop(0, blocks_q // 2, two, 0)
-
-    def keep(qb, part):
-        total[qb] = part
-
-    lax.fori_loop(0, len(inner) * 3, fill, 0)
-    products(inner, keep)
-    across[1].wait_recv()
-    onward[1].start()
-    for side in range(2):
-        second_halos[side].wait_recv()
-        take(1, side)
-        run(at + len(inner) + 2 + side)
-    onward[1].wait_recv()
-    lax.fori_loop(len(inner) * 3, planes * 3, fill, 0)
-
-    def cross(qb):
-        return remote(obuf.at[qb, 2 * unit : 4 * unit], relay.at[qb], out_sem.at[qb], vec=1 - v)
-
-    def along(qb, hop, ds):
-        root = (v if hop == 0 else 1 - v) * 2 + s
-        source = obuf if hop == 0 else relay
-        src = source.at[qb, ds * unit : (ds + 1) * unit]
-        dst = rx.at[qb, b]
-        sems = last_sem.at[qb]
-        far = pltpu.make_async_remote_copy(
+                        k = position[t] * 3 + c
+                        sr = smeared[k, 16 * h : 16 * h + 16, lane : lane + 256]
+                        si = smeared[k, 16 * h : 16 * h + 16, plane + lane : plane + lane + 256]
+                        col = (n * 3 + c) * wide + lane
+                        to[16 * j : 16 * j + 16, col : col + 256] = cosine * sr + sine * si
+                        to[16 * j : 16 * j + 16, col + plane : col + plane + 256] = cosine * si - sine * sr
+
+    def product(i):
+        h, half, qb = blocks[i]
+        columns = 16 * min(per, count - qb * per)
+        first = parts[half].start
+        length = parts[half].stop - first
+        pieces = []
+        for k in range(0, length, length // 2):
+            pieces.append(
+                lax.dot_general(
+                    right[:, first + k : first + k + length // 2],
+                    left[i % 2][0:columns, k : k + length // 2],
+                    (((1,), (1,)), ((), ())), preferred_element_type=f32,
+                )
+            )
+        if i + 1 < len(blocks) and not (blocks[i + 1][1] == 1 and blocks[i + 1][2] == 0):
+            turn(i + 1)
+        part = pieces[0] + pieces[1]
+        e = h * blocks_q + qb
+        if half == 0:
+            total[e, :, 0:columns] = part
+        else:
+            obuf[e, :, 0:columns] = ((total[e, :, 0:columns] + part) * scale).astype(low)
+
+    def cross(e):
+        return remote(obuf.at[e, 2 * unit : 4 * unit], relay.at[e], out_sem.at[e], vec=1 - v)
+
+    roots = (v * 2 + s, (1 - v) * 2 + s)
+
+    def ends(e, hop, ds):
+        source = relay if hop else obuf
+        return source.at[e, ds * unit : (ds + 1) * unit], rx.at[e, b], last_sem.at[e]
+
+    def far(e, hop, ds):
+        src, dst, sems = ends(e, hop, ds)
+        return pltpu.make_async_remote_copy(
             src_ref=src, dst_ref=dst, send_sem=sems.at[bricks + hop * 2 + ds], recv_sem=sems.at[b],
-            device_id={"brick": root, "sub": (s + ds) % 2}, device_id_type=pl.DeviceIdType.MESH,
-        )
-        near = pltpu.make_async_copy(src, dst, sems.at[b])
-        return root, far, near
-
-    def depart(qb, hop):
-        for ds in range(2):
-            root, far, near = along(qb, hop, ds)
-            if ds:
-                far.start()
-            else:
-                pl.when(root == b)(near.start)
-                pl.when(root != b)(far.start)
-
-    def hand_on(qb):
-        cross(qb).wait_recv()
-        depart(qb, 1)
-
-    def ship(qb, part):
-        obuf[qb] = ((total[qb] + part) * scale).astype(low)
-        cross(qb).start()
-        depart(qb, 0)
-        pl.when(qb > 0)(lambda: hand_on(qb - 1))
-
-    products(outer, ship)
-    hand_on(blocks_q - 1)
-    for qb in range(blocks_q):
+            device_id={"brick": roots[hop], "sub": (s + ds) % 2}, device_id_type=pl.DeviceIdType.MESH,
+        )
+
+    def depart(e, hop):
+        far(e, hop, 1).start()
+
+        @pl.when(roots[hop] != b)
+        def _():
+            far(e, hop, 0).start()
+
+        @pl.when(roots[hop] == b)
+        def _():
+            src, dst, sems = ends(e, hop, 0)
+            pltpu.make_async_copy(src, dst, sems.at[b]).start()
+
+    def hand_on(e):
+        cross(e).wait_recv()
+        depart(e, 1)
+
+    def ship(e):
+        cross(e).start()
+        depart(e, 0)
+        if e > 0:
+            hand_on(e - 1)
+
+    def fill_half(half):
+        first = len(inner) * 3 if half else 0
+        count_k = len(members[half]) * 3
+        lax.fori_loop(first, first + count_k, fill, 0)
+
+    for h in range(halves):
+        for half in range(2):
+            if half:
+                if h == 0:
+                    across[1].wait_recv()
+                    onward[1].start()
+                for side in range(2):
+                    take(1, h, side)
+                    run(1, [outer[side]], h)
+                if h == 0:
+                    onward[1].wait_recv()
+            if h == 0:
+                fill_half(half)
+            for qb in range(blocks_q):
+                i = blocks.index((h, half, qb))
+                if qb == 0 and (half or h == 0):
+                    turn(i)
+                product(i)
+                if half:
+                    ship(h * blocks_q + qb)
+    ships = halves * blocks_q
+    hand_on(ships - 1)
+    for e in range(ships):
         acc = None
         for i in range(bricks):
-            pltpu.make_async_copy(rx.at[qb, i], rx.at[qb, i], last_sem.at[qb, i]).wait()
-            got = rx[qb, i].astype(f32)
+            pltpu.make_async_copy(rx.at[e, i], rx.at[e, i], last_sem.at[e, i]).wait()
+            got = rx[e, i].astype(f32)
             acc = got if acc is None else acc + got
-        out_ref[:, qb * per * rows : (qb + 1) * per * rows] = acc
-    for copy in (links_up, *first_halos, *second_halos, *across, beside, *onward):
+        out_ref[:, e * per * 16 : (e + 1) * per * 16] = acc
+    sent = [links_up, *across, beside, *onward]
+    for copy in copies.values():
+        sent += copy
+    for copy in sent:
         copy.wait_send()
-    for qb in range(blocks_q):
-        cross(qb).wait_send()
+    for e in range(ships):
+        cross(e).wait_send()
         for hop in range(2):
-            for ds in range(2):
-                root, far, near = along(qb, hop, ds)
-                if ds:
-                    far.wait_send()
-                else:
-                    pl.when(root != b)(far.wait_send)
+            far(e, hop, 1).wait_send()
+
+            @pl.when(roots[hop] != b)
+            def _():
+                far(e, hop, 0).wait_send()
 
 
 def shards_fused(vectors, gauge_links, momenta):
@@ -544,8 +600,10 @@
     tiles = plane // 128
     bricks = lax.axis_size("brick")
     count = momenta.shape[0]
-    per = 256 // rows
-    blocks_q = 2 * (-(-count // (2 * per)))
+    per = 256 // 16
+    blocks_q = -(-count // per)
+    halves = rows // 16
+    ships = halves * blocks_q
     low, f32 = jnp.bfloat16, jnp.float32
     v = vectors.reshape((rows, 3, 2, planes * tiles, 128)).transpose((0, 1, 3, 2, 4))
     v = v.reshape((rows * 3, planes, tiles * 2, 128))
@@ -558,7 +616,7 @@
     plan = (planes, rows, count, bricks, per, blocks_q, scale)
     out = pl.pallas_call(
         functools.partial(fused_kernel, plan),
-        out_shape=jax.ShapeDtypeStruct((2 * rows, blocks_q * per * rows), f32),
+        out_shape=jax.ShapeDtypeStruct((2 * rows, ships * per * 16), f32),
         in_specs=[
             pl.BlockSpec(memory_space=pltpu.SMEM),
             pl.BlockSpec(memory_space=pl.ANY),
@@ -568,37 +626,39 @@
         scratch_shapes=[
             vmem((planes, rows * 3, tiles * 2, 128), f32),
             vmem((64 * planes * tiles, 128), f32),
-            vmem((2, planes + 2, 3, rows, wide), f32),
+            vmem((planes + 2, 3, rows, wide), f32),
+            vmem((planes + 2, 3, rows, wide), f32),
             vmem((planes + 1, 108, 8, plane), f32),
-            vmem((2, 4, 3, rows, wide), f32),
+            vmem((4, 3, 16, wide), f32),
+            vmem((4, 3, 16, wide), f32),
             vmem((8 * rows, planes * 3 * wide), low),
             vmem((planes * 3, rows, wide), low),
-            vmem((per * rows, most), low),
-            vmem((per * rows, most), low),
-            vmem((per * blocks_q, 16, local_sites), low),
-            vmem((per * blocks_q, 16, local_sites), low),
-            vmem((blocks_q, 8 * rows, per * rows), f32),
-            vmem((blocks_q, 8 * rows, per * rows), low),
-            vmem((blocks_q, 4 * rows, per * rows), low),
-            vmem((blocks_q, bricks, 2 * rows, per * rows), low),
-            vmem((2, 2, rows, 3 * wide), low),
-            vmem((2, rows, 3 * wide), low),
+            vmem((per * 16, most), low),
+            vmem((per * 16, most), low),
+            vmem((count, 16, local_sites), low),
+            vmem((count, 16, local_sites), low),
+            vmem((ships, 8 * rows, per * 16), f32),
+            vmem((ships, 8 * rows, per * 16), low),
+            vmem((ships, 4 * rows, per * 16), low),
+            vmem((ships, bricks, 2 * rows, per * 16), low),
+            vmem((2, halves, 2, 16, 3 * wide), low),
+            vmem((halves, 2, 16, 3 * wide), low),
             vmem((32, plane), low),
             vmem((32, plane), low),
             dma((planes + 1,)),
-            dma((2, 2, 2)),
+            dma((2, halves, 2, 2)),
             dma((2,)),
             dma((5, 2)),
-            dma((blocks_q, 2)),
-            dma((blocks_q, bricks + 4)),
+            dma((ships, 2)),
+            dma((ships, bricks + 4)),
         ],
         compiler_params=pltpu.CompilerParams(
             vmem_limit_bytes=60 * 2**20, collective_id=0, has_side_effects=True
         ),
         name="elementals",
     )(momenta.T, v, g)
-    out = out.reshape((2, rows, blocks_q * per, rows))[:, :, :count]
-    return jnp.transpose(out, (1, 2, 0, 3))
+    out = out.reshape((2, rows, halves, blocks_q * per, 16))[:, :, :, :count]
+    return jnp.transpose(out, (1, 3, 0, 2, 4)).reshape((rows, count, 2, rows))
 
 
 def choose(vectors, gauge_links, momenta):

time: 55 us -> 50.9 us (0.925)
  Pallas kernels: 51.6 us -> 47.1 us
  local copies, waits for them, and re-layouts: 2.9 us -> 3.61 us
    pallas_call x1, Pallas kernels: 51.6 us -> 47.1 us  [shards_fused(): pl.pallas_call(functools.partial(fused_kernel, plan), out_shape=jax.Shape...]
    unnamed x1 -> x0, local copies, waits for them, and re-layouts: 1.61 us -> none
    pallas_call x0 -> x1, local copies, waits for them, and re-layouts: none -> 1.14 us  [shards_fused(): pl.pallas_call(functools.partial(fused_kernel, plan), out_shape=jax.Shape...]
    reshape x1 -> x2, local copies, waits for them, and re-layouts: 1.29 us -> 2.3 us  [the longest x1 1.69 us: shards_fused(): return jnp.transpose(out, (1, 3, 0, 2, 4)).reshape((rows, count, 2, rows))]
where the time goes in v2:
time: 50.9 us; the launch traced here: 50.7 us
  Pallas kernels  47.1 us (93%)
  local copies, waits for them, and re-layouts  3.61 us (7%)
    pallas_call x1, Pallas kernels, shards_fused(): pl.pallas_call(functools.partial(fused_kernel, plan), out_shape=jax.Shape...  47.1 us
    reshape x1, local copies, waits for them, and re-layouts, shards_fused(): return jnp.transpose(out, (1, 3, 0, 2, 4)).reshape((rows, count, 2, rows))  1.69 us
    pallas_call x1, local copies, waits for them, and re-layouts, shards_fused(): pl.pallas_call(functools.partial(fused_kernel, plan), out_shape=jax.Shape...  1.14 us

profile of v2, /device:TPU:2, one launch (start us, length us, event | category | flops | bytes accessed | tf_op | source)
XLA Modules:
  0.0 50.7 jit_solution(9158165152715985823)
XLA Ops:
  0.0 47.1 %elementals.1 = f32[64,1024]{1,0:T(8,128)} custom-call(s32[3,27]{1,0:T(4,128)} %bitcast.19, f32[96,4,8,128]{3,2,1,0:T(8,128)} %bitcast.17, f32[864,128]{1,0:T(8,128)} %bitcast.18), custom_call_target="tpu_custom_call" | custom-call | tf_op jit(solution)/shard_map/elementals/pallas_call | solution.py:617
  47.1 1.1 %copy.9 = f32[64,1024]{0,1:T(8,128)S(1)} copy(f32[64,1024]{1,0:T(8,128)} %elementals.1) | data formatting | bytes 524288 | tf_op jit(solution)/shard_map/elementals/pallas_call | solution.py:617
  48.2 0.6 %reshape.22 = f32[2,32,2,32,16]{1,0,4,3,2:T(2,128)S(1)} reshape(f32[64,1024]{0,1:T(8,128)S(1)} %copy.9) | data formatting | bytes 524288 | tf_op jit(solution)/shard_map/reshape | solution.py:660
  48.8 0.1 slice_bitcast_fusion
  48.9 0.1 copy.10
  49.0 1.7 %copy.11 = f32[32,27,2,32]{3,2,1,0:T(2,128)} copy(f32[32,27,2,32]{0,3,2,1:T(8,128)S(1)} %bitcast.16) | data formatting | bytes 442368 | tf_op jit(solution)/shard_map/reshape | solution.py:661

commit v3 on v2

--- a/solution.py
+++ b/solution.py
@@ -150,9 +150,9 @@
 
 
 def fused_kernel(plan, mom_ref, v_ref, g_ref, out_ref, *scratch):
-    (vst, gst, field0, field1, table, moved0, moved1, right, smeared, left0, left1, cosb, sinb, total, obuf,
-     relay, rx, halo, hsend, lsend, lrecv, load_sem, halo_sem, link_sem, raw_sem, out_sem, last_sem) = scratch
-    planes, rows, count, bricks, per, blocks_q, scale = plan
+    (vst, gst, field0, field1, table, moved0, moved1, right, smeared, left0, left1, cosb, sinb, total, parted,
+     crossing, paired, summed, rx, halo, hsend, lsend, lrecv, load_sem, halo_sem, link_sem, raw_sem, cross_sem, pair_sem, last_sem) = scratch
+    planes, rows, count, bricks, units, scale = plan
     fields, moved = (field0, field1), (moved0, moved1)
     halves = rows // 16
     plane = LY * LZ
@@ -414,8 +414,7 @@
             i = stages.index((step, t, h))
 
             def trip(k, carry):
-                if i + 1 < len(stages):
-                    shift(stages[i + 1], k, moved[(i + 1) % 2])
+                shift(stages[(i + 1) % len(stages)], k, moved[(i + 1) % 2])
                 block(stages[i], k, moved[i % 2])
                 return carry
 
@@ -463,14 +462,15 @@
             right[at_turned, im] = right[at_raw, re]
         return carry
 
-    blocks = [(h, half, qb) for h in range(halves) for half in range(2) for qb in range(blocks_q)]
+    ships = len(units)
     members = (inner, outer)
+    order = [(half, e) for group in (range(0, 2), range(2, ships)) for half in range(2) for e in group]
+    ready = lambda i: not (order[i][0] == 1 and order[i - 1][0] == 0)
 
     def turn(i):
-        h, half, qb = blocks[i]
+        half, e = order[i]
         to = left[i % 2]
-        for j in range(min(per, count - qb * per)):
-            q = qb * per + j
+        for j, (q, h) in enumerate(units[e]):
             for n, t in enumerate(members[half]):
                 for lane in range(0, plane, 256):
                     cosine = cosb[q, :, t * plane + lane : t * plane + lane + 256]
@@ -484,8 +484,8 @@
                         to[16 * j : 16 * j + 16, col + plane : col + plane + 256] = cosine * si - sine * sr
 
     def product(i):
-        h, half, qb = blocks[i]
-        columns = 16 * min(per, count - qb * per)
+        half, e = order[i]
+        columns = 16 * len(units[e])
         first = parts[half].start
         length = parts[half].stop - first
         pieces = []
@@ -497,100 +497,146 @@
                     (((1,), (1,)), ((), ())), preferred_element_type=f32,
                 )
             )
-        if i + 1 < len(blocks) and not (blocks[i + 1][1] == 1 and blocks[i + 1][2] == 0):
+        if i + 1 < len(order) and ready(i + 1):
             turn(i + 1)
         part = pieces[0] + pieces[1]
-        e = h * blocks_q + qb
         if half == 0:
             total[e, :, 0:columns] = part
         else:
-            obuf[e, :, 0:columns] = ((total[e, :, 0:columns] + part) * scale).astype(low)
+            part = ((total[e, :, 0:columns] + part) * scale).astype(low)
+            parted[e, 0, :, 0:columns] = part[0 : 2 * unit]
+            crossing[e, :, 0:columns] = part[2 * unit :]
+
+    sizes = [128 * (-(-len(u) // 8)) for u in units]
+    keeper = b % 2 == s
+    pair_brick = b + 1 - 2 * (b % 2)
+    far_brick = (b + 2) % 4
+    near_hop = (v + b // 2) % 2
 
     def cross(e):
-        return remote(obuf.at[e, 2 * unit : 4 * unit], relay.at[e], out_sem.at[e], vec=1 - v)
-
-    roots = (v * 2 + s, (1 - v) * 2 + s)
-
-    def ends(e, hop, ds):
-        source = relay if hop else obuf
-        return source.at[e, ds * unit : (ds + 1) * unit], rx.at[e, b], last_sem.at[e]
-
-    def far(e, hop, ds):
-        src, dst, sems = ends(e, hop, ds)
+        return remote(
+            crossing.at[e, :, 0 : sizes[e]], parted.at[e, 1, :, 0 : sizes[e]], cross_sem.at[e], vec=1 - v
+        )
+
+    def pair_up(e, hop):
+        return remote(
+            parted.at[e, hop, :, 0 : sizes[e]], paired.at[e, hop, :, 0 : sizes[e]],
+            pair_sem.at[e, hop], brick=pair_brick,
+        )
+
+    def deliver(e, far, ds):
+        src = summed.at[e, far, ds * unit : (ds + 1) * unit, 0 : sizes[e]]
+        ids = {"brick": far_brick} if far else {}
+        if ds:
+            ids["sub"] = 1 - s
         return pltpu.make_async_remote_copy(
-            src_ref=src, dst_ref=dst, send_sem=sems.at[bricks + hop * 2 + ds], recv_sem=sems.at[b],
-            device_id={"brick": roots[hop], "sub": (s + ds) % 2}, device_id_type=pl.DeviceIdType.MESH,
-        )
-
-    def depart(e, hop):
-        far(e, hop, 1).start()
-
-        @pl.when(roots[hop] != b)
+            src_ref=src, dst_ref=rx.at[e, far, :, 0 : sizes[e]],
+            send_sem=last_sem.at[e, 2 * far + ds], recv_sem=last_sem.at[e, 4 + far],
+            device_id=ids, device_id_type=pl.DeviceIdType.MESH,
+        )
+
+    def ship(e):
+        cross(e).start()
+
+        @pl.when(jnp.logical_not(keeper))
         def _():
-            far(e, hop, 0).start()
-
-        @pl.when(roots[hop] == b)
-        def _():
-            src, dst, sems = ends(e, hop, 0)
-            pltpu.make_async_copy(src, dst, sems.at[b]).start()
+            pair_up(e, 0).start()
 
     def hand_on(e):
         cross(e).wait_recv()
-        depart(e, 1)
-
-    def ship(e):
-        cross(e).start()
-        depart(e, 0)
-        if e > 0:
-            hand_on(e - 1)
+
+        @pl.when(jnp.logical_not(keeper))
+        def _():
+            pair_up(e, 1).start()
+
+    def combine(e):
+        @pl.when(keeper)
+        def _():
+            for hop in range(2):
+                pair_up(e, hop).wait_recv()
+            for far in (1, 0):
+                hop = 1 - near_hop if far else near_hop
+                both = parted[e, hop, :, 0 : sizes[e]].astype(f32) + paired[e, hop, :, 0 : sizes[e]].astype(f32)
+                summed[e, far, :, 0 : sizes[e]] = both.astype(low)
+                if far == 0:
+                    rx[e, 0, :, 0 : sizes[e]] = both[0:unit].astype(low)
+            deliver(e, 1, 0).start()
+            deliver(e, 1, 1).start()
+            deliver(e, 0, 1).start()
+
+    def arrive(e):
+        @pl.when(jnp.logical_not(keeper))
+        def _():
+            deliver(e, 0, 1).wait_recv()
+
+        deliver(e, 1, 0).wait_recv()
 
     def fill_half(half):
         first = len(inner) * 3 if half else 0
         count_k = len(members[half]) * 3
         lax.fori_loop(first, first + count_k, fill, 0)
 
-    for h in range(halves):
-        for half in range(2):
-            if half:
-                if h == 0:
-                    across[1].wait_recv()
-                    onward[1].start()
-                for side in range(2):
-                    take(1, h, side)
-                    run(1, [outer[side]], h)
-                if h == 0:
-                    onward[1].wait_recv()
-            if h == 0:
-                fill_half(half)
-            for qb in range(blocks_q):
-                i = blocks.index((h, half, qb))
-                if qb == 0 and (half or h == 0):
-                    turn(i)
-                product(i)
-                if half:
-                    ship(h * blocks_q + qb)
-    ships = halves * blocks_q
-    hand_on(ships - 1)
+    hooks = {
+        2: [(ship, 0)],
+        3: [(ship, 1), (hand_on, 0)],
+        4: [(hand_on, 1), (combine, 0)],
+        5: [(combine, 1)],
+        6: [(ship, 2)],
+        7: [(ship, 3), (hand_on, 2), (combine, 2), (hand_on, 3), (combine, 3)],
+    }
+    for i, (half, e) in enumerate(order):
+        if i == 0:
+            fill_half(0)
+        if i == 2:
+            across[1].wait_recv()
+            onward[1].start()
+        if i in (2, 6):
+            for side in range(2):
+                take(1, i // 4, side)
+                run(1, [outer[side]], i // 4)
+        if i == 2:
+            onward[1].wait_recv()
+            fill_half(1)
+        if i == 0 or not ready(i):
+            turn(i)
+        product(i)
+        for act, which in hooks.get(i, ()):
+            act(which)
+    lane_at = lax.broadcasted_iota(jnp.int32, (8, 128), 1)
+    places = {pair: (e, 16 * j) for e, u in enumerate(units) for j, pair in enumerate(u)}
     for e in range(ships):
-        acc = None
-        for i in range(bricks):
-            pltpu.make_async_copy(rx.at[e, i], rx.at[e, i], last_sem.at[e, i]).wait()
-            got = rx[e, i].astype(f32)
-            acc = got if acc is None else acc + got
-        out_ref[:, e * per * 16 : (e + 1) * per * 16] = acc
+        arrive(e)
+    for q in range(count):
+        for first in range(0, unit, 8):
+            pieces = []
+            for h in range(halves):
+                e, at = places[q, h]
+                tile = slice(at // 128 * 128, at // 128 * 128 + 128)
+                rows_at = slice(first // 16 * 16, first // 16 * 16 + 16)
+                got = rx[e, 0, rows_at, tile].astype(f32) + rx[e, 1, rows_at, tile].astype(f32)
+                got = got[first % 16 : first % 16 + 8]
+                turned = (16 * h - at) % 128
+                pieces.append(pltpu.roll(got, turned, 1) if turned else got)
+            value = jnp.where(lane_at < 16, pieces[0], pieces[1])
+            start = (first % rows) * 2 * count + 2 * q + first // rows
+            out_ref[pl.ds(start, 8, stride=2 * count), :] = value[:, 0:rows]
     sent = [links_up, *across, beside, *onward]
     for copy in copies.values():
         sent += copy
+    sent += [cross(e) for e in range(ships)]
     for copy in sent:
         copy.wait_send()
     for e in range(ships):
-        cross(e).wait_send()
-        for hop in range(2):
-            far(e, hop, 1).wait_send()
-
-            @pl.when(roots[hop] != b)
-            def _():
-                far(e, hop, 0).wait_send()
+        @pl.when(keeper)
+        def _():
+            deliver(e, 1, 0).wait_send()
+            deliver(e, 1, 1).wait_send()
+            deliver(e, 0, 1).wait_send()
+
+        @pl.when(jnp.logical_not(keeper))
+        def _():
+            pair_up(e, 0).wait_send()
+            pair_up(e, 1).wait_send()
 
 
 def shards_fused(vectors, gauge_links, momenta):
@@ -600,10 +646,14 @@
     tiles = plane // 128
     bricks = lax.axis_size("brick")
     count = momenta.shape[0]
-    per = 256 // 16
-    blocks_q = -(-count // per)
     halves = rows // 16
-    ships = halves * blocks_q
+    even = count // 8 * 8
+    split = even * 2 // 3 // 8 * 8
+    units = [[(q, 0) for q in range(split)], [(q, 0) for q in range(split, even)]]
+    units += [[(q, 1) for q in range(split)], [(q, 1) for q in range(split, even)]]
+    units[3] += [(q, h) for q in range(even, count) for h in range(halves)]
+    ships, most_units = len(units), max(len(u) for u in units)
+    width = 128 * (-(-most_units // 8))
     low, f32 = jnp.bfloat16, jnp.float32
     v = vectors.reshape((rows, 3, 2, planes * tiles, 128)).transpose((0, 1, 3, 2, 4))
     v = v.reshape((rows * 3, planes, tiles * 2, 128))
@@ -613,10 +663,10 @@
     most = max(2, planes - 2) * 3 * wide
     scale = (3.0 * bricks * local_sites) ** (-0.5)
     vmem, dma = pltpu.VMEM, pltpu.SemaphoreType.DMA
-    plan = (planes, rows, count, bricks, per, blocks_q, scale)
+    plan = (planes, rows, count, bricks, units, scale)
     out = pl.pallas_call(
         functools.partial(fused_kernel, plan),
-        out_shape=jax.ShapeDtypeStruct((2 * rows, ships * per * 16), f32),
+        out_shape=jax.ShapeDtypeStruct((rows * count * 2, rows), f32),
         in_specs=[
             pl.BlockSpec(memory_space=pltpu.SMEM),
             pl.BlockSpec(memory_space=pl.ANY),
@@ -633,14 +683,16 @@
             vmem((4, 3, 16, wide), f32),
             vmem((8 * rows, planes * 3 * wide), low),
             vmem((planes * 3, rows, wide), low),
-            vmem((per * 16, most), low),
-            vmem((per * 16, most), low),
+            vmem((16 * most_units, most), low),
+            vmem((16 * most_units, most), low),
             vmem((count, 16, local_sites), low),
             vmem((count, 16, local_sites), low),
-            vmem((ships, 8 * rows, per * 16), f32),
-            vmem((ships, 8 * rows, per * 16), low),
-            vmem((ships, 4 * rows, per * 16), low),
-            vmem((ships, bricks, 2 * rows, per * 16), low),
+            vmem((ships, 8 * rows, width), f32),
+            vmem((ships, 2, 4 * rows, width), low),
+            vmem((ships, 4 * rows, width), low),
+            vmem((ships, 2, 4 * rows, width), low),
+            vmem((ships, 2, 4 * rows, width), low),
+            vmem((ships, 2, 2 * rows, width), low),
             vmem((2, halves, 2, 16, 3 * wide), low),
             vmem((halves, 2, 16, 3 * wide), low),
             vmem((32, plane), low),
@@ -650,15 +702,15 @@
             dma((2,)),
             dma((5, 2)),
             dma((ships, 2)),
-            dma((ships, bricks + 4)),
+            dma((ships, 2, 2)),
+            dma((ships, 6)),
         ],
         compiler_params=pltpu.CompilerParams(
             vmem_limit_bytes=60 * 2**20, collective_id=0, has_side_effects=True
         ),
         name="elementals",
     )(momenta.T, v, g)
-    out = out.reshape((2, rows, halves, blocks_q * per, 16))[:, :, :, :count]
-    return jnp.transpose(out, (1, 3, 0, 2, 4)).reshape((rows, count, 2, rows))
+    return out.reshape((rows, count, 2, rows))
 
 
 def choose(vectors, gauge_links, momenta):
@@ -666,7 +718,7 @@
     bricks, vecs, subs = (lax.axis_size(a) for a in ("brick", "vec", "sub"))
     rows, local_sites = vectors.shape[0], vectors.shape[3]
     fits = local_sites % plane == 0 and 3 <= local_sites // plane <= 4 and rows == 32
-    if fits and vecs == 2 and subs == 2 and bricks == 4:
+    if fits and vecs == 2 and subs == 2 and bricks == 4 and 24 <= momenta.shape[0] < 32:
         return shards_fused(vectors, gauge_links, momenta)
     return shards(vectors, gauge_links, momenta)
 

time: 50.9 us -> 55.3 us (1.086)
  the two profiles are of different devices: /device:TPU:2 before, /device:TPU:0 now
where the time goes in v3:
time: 55.3 us; the launch traced here: 55.1 us
  Pallas kernels  53 us (96%)
  local copies, waits for them, and re-layouts  2.15 us (4%)
    pallas_call x1, Pallas kernels, shards_fused(): pl.pallas_call(functools.partial(fused_kernel, plan), out_shape=jax.Shape...  53 us
    unnamed x1, local copies, waits for them, and re-layouts  2.15 us

profile of v3, /device:TPU:0, one launch (start us, length us, event | category | flops | bytes accessed | tf_op | source)
XLA Modules:
  0.0 55.1 jit_solution(1491528830168727925)
XLA Ops:
  0.0 53.0 %elementals.1 = f32[1728,32]{1,0:T(8,128)} custom-call(s32[3,27]{1,0:T(4,128)} %bitcast.15, f32[96,4,8,128]{3,2,1,0:T(8,128)} %bitcast.13, f32[864,128]{1,0:T(8,128)} %bitcast.14), custom_call_target="tpu_custom_call" | custom-call | tf_op jit(solution)/shard_map/elementals/pallas_call | solution.py:667
  53.0 2.2 %copy.7 = f32[32,27,2,32]{3,2,1,0:T(2,128)} copy(f32[32,27,2,32]{3,2,1,0:T(2,128)} %bitcast.12) | data formatting | bytes 442368

commit v4 on v3

--- a/solution.py
+++ b/solution.py
@@ -151,7 +151,7 @@
 
 def fused_kernel(plan, mom_ref, v_ref, g_ref, out_ref, *scratch):
     (vst, gst, field0, field1, table, moved0, moved1, right, smeared, left0, left1, cosb, sinb, total, parted,
-     crossing, paired, summed, rx, halo, hsend, lsend, lrecv, load_sem, halo_sem, link_sem, raw_sem, cross_sem, pair_sem, last_sem) = scratch
+     crossing, rx, halo, hsend, lsend, lrecv, load_sem, halo_sem, link_sem, raw_sem, cross_sem, last_sem) = scratch
     planes, rows, count, bricks, units, scale = plan
     fields, moved = (field0, field1), (moved0, moved1)
     halves = rows // 16
@@ -499,77 +499,58 @@
             )
         if i + 1 < len(order) and ready(i + 1):
             turn(i + 1)
-        part = pieces[0] + pieces[1]
+        part = pieces[0] * scale + pieces[1] * scale
         if half == 0:
             total[e, :, 0:columns] = part
         else:
-            part = ((total[e, :, 0:columns] + part) * scale).astype(low)
+            part = (total[e, :, 0:columns] + part).astype(low)
             parted[e, 0, :, 0:columns] = part[0 : 2 * unit]
             crossing[e, :, 0:columns] = part[2 * unit :]
 
     sizes = [128 * (-(-len(u) // 8)) for u in units]
-    keeper = b % 2 == s
-    pair_brick = b + 1 - 2 * (b % 2)
-    far_brick = (b + 2) % 4
-    near_hop = (v + b // 2) % 2
+    roots = (v * 2 + s, (1 - v) * 2 + s)
 
     def cross(e):
         return remote(
             crossing.at[e, :, 0 : sizes[e]], parted.at[e, 1, :, 0 : sizes[e]], cross_sem.at[e], vec=1 - v
         )
 
-    def pair_up(e, hop):
-        return remote(
-            parted.at[e, hop, :, 0 : sizes[e]], paired.at[e, hop, :, 0 : sizes[e]],
-            pair_sem.at[e, hop], brick=pair_brick,
-        )
-
-    def deliver(e, far, ds):
-        src = summed.at[e, far, ds * unit : (ds + 1) * unit, 0 : sizes[e]]
-        ids = {"brick": far_brick} if far else {}
-        if ds:
-            ids["sub"] = 1 - s
+    def ends(e, hop, ds):
+        src = parted.at[e, hop, ds * unit : (ds + 1) * unit, 0 : sizes[e]]
+        return src, rx.at[e, b, :, 0 : sizes[e]]
+
+    def far(e, hop, ds):
+        src, dst = ends(e, hop, ds)
         return pltpu.make_async_remote_copy(
-            src_ref=src, dst_ref=rx.at[e, far, :, 0 : sizes[e]],
-            send_sem=last_sem.at[e, 2 * far + ds], recv_sem=last_sem.at[e, 4 + far],
-            device_id=ids, device_id_type=pl.DeviceIdType.MESH,
-        )
+            src_ref=src, dst_ref=dst,
+            send_sem=last_sem.at[e, bricks + hop * 2 + ds], recv_sem=last_sem.at[e, b],
+            device_id={"brick": roots[hop], "sub": (s + ds) % 2}, device_id_type=pl.DeviceIdType.MESH,
+        )
+
+    def depart(e, hop):
+        far(e, hop, 1).start()
+
+        @pl.when(roots[hop] != b)
+        def _():
+            far(e, hop, 0).start()
+
+        @pl.when(roots[hop] == b)
+        def _():
+            src, dst = ends(e, hop, 0)
+            pltpu.make_async_copy(src, dst, last_sem.at[e, b]).start()
 
     def ship(e):
         cross(e).start()
-
-        @pl.when(jnp.logical_not(keeper))
-        def _():
-            pair_up(e, 0).start()
+        depart(e, 0)
 
     def hand_on(e):
         cross(e).wait_recv()
-
-        @pl.when(jnp.logical_not(keeper))
-        def _():
-            pair_up(e, 1).start()
-
-    def combine(e):
-        @pl.when(keeper)
-        def _():
-            for hop in range(2):
-                pair_up(e, hop).wait_recv()
-            for far in (1, 0):
-                hop = 1 - near_hop if far else near_hop
-                both = parted[e, hop, :, 0 : sizes[e]].astype(f32) + paired[e, hop, :, 0 : sizes[e]].astype(f32)
-                summed[e, far, :, 0 : sizes[e]] = both.astype(low)
-                if far == 0:
-                    rx[e, 0, :, 0 : sizes[e]] = both[0:unit].astype(low)
-            deliver(e, 1, 0).start()
-            deliver(e, 1, 1).start()
-            deliver(e, 0, 1).start()
+        depart(e, 1)
 
     def arrive(e):
-        @pl.when(jnp.logical_not(keeper))
-        def _():
-            deliver(e, 0, 1).wait_recv()
-
-        deliver(e, 1, 0).wait_recv()
+        for i in range(bricks):
+            dst = rx.at[e, i, :, 0 : sizes[e]]
+            pltpu.make_async_copy(dst, dst, last_sem.at[e, i]).wait()
 
     def fill_half(half):
         first = len(inner) * 3 if half else 0
@@ -579,10 +560,9 @@
     hooks = {
         2: [(ship, 0)],
         3: [(ship, 1), (hand_on, 0)],
-        4: [(hand_on, 1), (combine, 0)],
-        5: [(combine, 1)],
+        4: [(hand_on, 1)],
         6: [(ship, 2)],
-        7: [(ship, 3), (hand_on, 2), (combine, 2), (hand_on, 3), (combine, 3)],
+        7: [(ship, 3), (hand_on, 2), (hand_on, 3)],
     }
     for i, (half, e) in enumerate(order):
         if i == 0:
@@ -613,7 +593,8 @@
                 e, at = places[q, h]
                 tile = slice(at // 128 * 128, at // 128 * 128 + 128)
                 rows_at = slice(first // 16 * 16, first // 16 * 16 + 16)
-                got = rx[e, 0, rows_at, tile].astype(f32) + rx[e, 1, rows_at, tile].astype(f32)
+                got = [rx[e, i, rows_at, tile].astype(f32) for i in range(bricks)]
+                got = (got[0] + got[1]) + (got[2] + got[3])
                 got = got[first % 16 : first % 16 + 8]
                 turned = (16 * h - at) % 128
                 pieces.append(pltpu.roll(got, turned, 1) if turned else got)
@@ -627,16 +608,12 @@
     for copy in sent:
         copy.wait_send()
     for e in range(ships):
-        @pl.when(keeper)
-        def _():
-            deliver(e, 1, 0).wait_send()
-            deliver(e, 1, 1).wait_send()
-            deliver(e, 0, 1).wait_send()
-
-        @pl.when(jnp.logical_not(keeper))
-        def _():
-            pair_up(e, 0).wait_send()
-            pair_up(e, 1).wait_send()
+        for hop in range(2):
+            far(e, hop, 1).wait_send()
+
+            @pl.when(roots[hop] != b)
+            def _():
+                far(e, hop, 0).wait_send()
 
 
 def shards_fused(vectors, gauge_links, momenta):
@@ -690,9 +667,7 @@
             vmem((ships, 8 * rows, width), f32),
             vmem((ships, 2, 4 * rows, width), low),
             vmem((ships, 4 * rows, width), low),
-            vmem((ships, 2, 4 * rows, width), low),
-            vmem((ships, 2, 4 * rows, width), low),
-            vmem((ships, 2, 2 * rows, width), low),
+            vmem((ships, bricks, 2 * rows, width), low),
             vmem((2, halves, 2, 16, 3 * wide), low),
             vmem((halves, 2, 16, 3 * wide), low),
             vmem((32, plane), low),
@@ -702,8 +677,7 @@
             dma((2,)),
             dma((5, 2)),
             dma((ships, 2)),
-            dma((ships, 2, 2)),
-            dma((ships, 6)),
+            dma((ships, bricks + 4)),
         ],
         compiler_params=pltpu.CompilerParams(
             vmem_limit_bytes=60 * 2**20, collective_id=0, has_side_effects=True

time: 55.3 us -> 49.4 us (0.89)
  the two profiles are of different devices: /device:TPU:0 before, /device:TPU:2 now
where the time goes in v4:
time: 49.4 us; the launch traced here: 49.2 us
  Pallas kernels  47.1 us (95%)
  local copies, waits for them, and re-layouts  2.15 us (4%)
    pallas_call x1, Pallas kernels, shards_fused(): pl.pallas_call(functools.partial(fused_kernel, plan), out_shape=jax.Shape...  47.1 us
    unnamed x1, local copies, waits for them, and re-layouts  2.15 us

profile of v4, /device:TPU:2, one launch (start us, length us, event | category | flops | bytes accessed | tf_op | source)
XLA Modules:
  0.0 49.2 jit_solution(16087054182626380210)
XLA Ops:
  0.0 47.1 %elementals.1 = f32[1728,32]{1,0:T(8,128)} custom-call(s32[3,27]{1,0:T(4,128)} %bitcast.15, f32[96,4,8,128]{3,2,1,0:T(8,128)} %bitcast.13, f32[864,128]{1,0:T(8,128)} %bitcast.14), custom_call_target="tpu_custom_call" | custom-call | tf_op jit(solution)/shard_map/elementals/pallas_call | solution.py:644
  47.1 2.2 %copy.7 = f32[32,27,2,32]{3,2,1,0:T(2,128)} copy(f32[32,27,2,32]{3,2,1,0:T(2,128)} %bitcast.12) | data formatting | bytes 442368

commit v5 on v4

--- a/solution.py
+++ b/solution.py
@@ -152,7 +152,7 @@
 def fused_kernel(plan, mom_ref, v_ref, g_ref, out_ref, *scratch):
     (vst, gst, field0, field1, table, moved0, moved1, right, smeared, left0, left1, cosb, sinb, total, parted,
      crossing, rx, halo, hsend, lsend, lrecv, load_sem, halo_sem, link_sem, raw_sem, cross_sem, last_sem) = scratch
-    planes, rows, count, bricks, units, scale = plan
+    planes, rows, count, bricks, ships, width, scale = plan
     fields, moved = (field0, field1), (moved0, moved1)
     halves = rows // 16
     plane = LY * LZ
@@ -462,62 +462,67 @@
             right[at_turned, im] = right[at_raw, re]
         return carry
 
-    ships = len(units)
     members = (inner, outer)
-    order = [(half, e) for group in (range(0, 2), range(2, ships)) for half in range(2) for e in group]
-    ready = lambda i: not (order[i][0] == 1 and order[i - 1][0] == 0)
+    order = [(h, half, t) for h in range(halves) for half in range(2) for t in members[half]]
+    per = width // 16
+    streamed = 16 * count
+
+    def ready(i):
+        return order[i][1] == 0 or order[i - 1][1] == 1
 
     def turn(i):
-        half, e = order[i]
+        h, half, t = order[i]
         to = left[i % 2]
-        for j, (q, h) in enumerate(units[e]):
-            for n, t in enumerate(members[half]):
-                for lane in range(0, plane, 256):
-                    cosine = cosb[q, :, t * plane + lane : t * plane + lane + 256]
-                    sine = sinb[q, :, t * plane + lane : t * plane + lane + 256]
-                    for c in range(3):
-                        k = position[t] * 3 + c
-                        sr = smeared[k, 16 * h : 16 * h + 16, lane : lane + 256]
-                        si = smeared[k, 16 * h : 16 * h + 16, plane + lane : plane + lane + 256]
-                        col = (n * 3 + c) * wide + lane
-                        to[16 * j : 16 * j + 16, col : col + 256] = cosine * sr + sine * si
-                        to[16 * j : 16 * j + 16, col + plane : col + plane + 256] = cosine * si - sine * sr
+        for q in range(count):
+            for lane in range(0, plane, 256):
+                cosine = cosb[q, :, t * plane + lane : t * plane + lane + 256]
+                sine = sinb[q, :, t * plane + lane : t * plane + lane + 256]
+                for c in range(3):
+                    k = position[t] * 3 + c
+                    sr = smeared[k, 16 * h : 16 * h + 16, lane : lane + 256]
+                    si = smeared[k, 16 * h : 16 * h + 16, plane + lane : plane + lane + 256]
+                    col = c * wide + lane
+                    to[16 * q : 16 * q + 16, col : col + 256] = cosine * sr + sine * si
+                    to[16 * q : 16 * q + 16, col + plane : col + plane + 256] = cosine * si - sine * sr
 
     def product(i):
-        half, e = order[i]
-        columns = 16 * len(units[e])
-        first = parts[half].start
-        length = parts[half].stop - first
+        h, half, t = order[i]
+        first = position[t] * 3 * wide
+        length = 3 * wide
         pieces = []
         for k in range(0, length, length // 2):
             pieces.append(
                 lax.dot_general(
+                    left[i % 2][:, k : k + length // 2],
                     right[:, first + k : first + k + length // 2],
-                    left[i % 2][0:columns, k : k + length // 2],
                     (((1,), (1,)), ((), ())), preferred_element_type=f32,
                 )
             )
         if i + 1 < len(order) and ready(i + 1):
             turn(i + 1)
         part = pieces[0] * scale + pieces[1] * scale
-        if half == 0:
-            total[e, :, 0:columns] = part
+        if t == inner[0]:
+            total[h, 0:streamed] = part
         else:
-            part = (total[e, :, 0:columns] + part).astype(low)
-            parted[e, 0, :, 0:columns] = part[0 : 2 * unit]
-            crossing[e, :, 0:columns] = part[2 * unit :]
-
-    sizes = [128 * (-(-len(u) // 8)) for u in units]
+            total[h, 0:streamed] += part
+
+    def finish(e):
+        per_half = ships // halves
+        at = e % per_half * width
+        part = total[e // per_half, at : at + width, :].T.astype(low)
+        parted[e, 0] = part[0 : 2 * unit]
+        crossing[e] = part[2 * unit :]
+
     roots = (v * 2 + s, (1 - v) * 2 + s)
 
     def cross(e):
         return remote(
-            crossing.at[e, :, 0 : sizes[e]], parted.at[e, 1, :, 0 : sizes[e]], cross_sem.at[e], vec=1 - v
+            crossing.at[e], parted.at[e, 1], cross_sem.at[e], vec=1 - v
         )
 
     def ends(e, hop, ds):
-        src = parted.at[e, hop, ds * unit : (ds + 1) * unit, 0 : sizes[e]]
-        return src, rx.at[e, b, :, 0 : sizes[e]]
+        src = parted.at[e, hop, ds * unit : (ds + 1) * unit]
+        return src, rx.at[e, b]
 
     def far(e, hop, ds):
         src, dst = ends(e, hop, ds)
@@ -540,6 +545,7 @@
             pltpu.make_async_copy(src, dst, last_sem.at[e, b]).start()
 
     def ship(e):
+        finish(e)
         cross(e).start()
         depart(e, 0)
 
@@ -549,7 +555,7 @@
 
     def arrive(e):
         for i in range(bricks):
-            dst = rx.at[e, i, :, 0 : sizes[e]]
+            dst = rx.at[e, i]
             pltpu.make_async_copy(dst, dst, last_sem.at[e, i]).wait()
 
     def fill_half(half):
@@ -557,40 +563,40 @@
         count_k = len(members[half]) * 3
         lax.fori_loop(first, first + count_k, fill, 0)
 
-    hooks = {
-        2: [(ship, 0)],
-        3: [(ship, 1), (hand_on, 0)],
-        4: [(hand_on, 1)],
-        6: [(ship, 2)],
-        7: [(ship, 3), (hand_on, 2), (hand_on, 3)],
-    }
-    for i, (half, e) in enumerate(order):
+    per_half = ships // halves
+    for i, (h, half, t) in enumerate(order):
+        opens = t == members[half][0]
         if i == 0:
             fill_half(0)
-        if i == 2:
-            across[1].wait_recv()
-            onward[1].start()
-        if i in (2, 6):
+        if half and opens:
+            if h == 0:
+                across[1].wait_recv()
+                onward[1].start()
             for side in range(2):
-                take(1, i // 4, side)
-                run(1, [outer[side]], i // 4)
-        if i == 2:
-            onward[1].wait_recv()
-            fill_half(1)
+                take(1, h, side)
+                run(1, [outer[side]], h)
+            if h == 0:
+                onward[1].wait_recv()
+                fill_half(1)
         if i == 0 or not ready(i):
             turn(i)
         product(i)
-        for act, which in hooks.get(i, ()):
-            act(which)
+        if h and not half and opens:
+            for e in range(per_half * (h - 1), per_half * h):
+                hand_on(e)
+        if half and not opens:
+            for e in range(per_half * h, per_half * (h + 1)):
+                ship(e)
+    for e in range(per_half * (halves - 1), ships):
+        hand_on(e)
     lane_at = lax.broadcasted_iota(jnp.int32, (8, 128), 1)
-    places = {pair: (e, 16 * j) for e, u in enumerate(units) for j, pair in enumerate(u)}
     for e in range(ships):
         arrive(e)
     for q in range(count):
         for first in range(0, unit, 8):
             pieces = []
             for h in range(halves):
-                e, at = places[q, h]
+                e, at = h * per_half + q // per, q % per * 16
                 tile = slice(at // 128 * 128, at // 128 * 128 + 128)
                 rows_at = slice(first // 16 * 16, first // 16 * 16 + 16)
                 got = [rx[e, i, rows_at, tile].astype(f32) for i in range(bricks)]
@@ -624,23 +630,18 @@
     bricks = lax.axis_size("brick")
     count = momenta.shape[0]
     halves = rows // 16
-    even = count // 8 * 8
-    split = even * 2 // 3 // 8 * 8
-    units = [[(q, 0) for q in range(split)], [(q, 0) for q in range(split, even)]]
-    units += [[(q, 1) for q in range(split)], [(q, 1) for q in range(split, even)]]
-    units[3] += [(q, h) for q in range(even, count) for h in range(halves)]
-    ships, most_units = len(units), max(len(u) for u in units)
-    width = 128 * (-(-most_units // 8))
+    width = 256
+    per_half = -(-count * 16 // width)
+    ships = halves * per_half
     low, f32 = jnp.bfloat16, jnp.float32
     v = vectors.reshape((rows, 3, 2, planes * tiles, 128)).transpose((0, 1, 3, 2, 4))
     v = v.reshape((rows * 3, planes, tiles * 2, 128))
     g = gauge_links.reshape((27, 2, planes * tiles, 128)).transpose((0, 2, 1, 3))
     g = g.reshape((54 * planes * tiles, 128))
     wide = 2 * plane
-    most = max(2, planes - 2) * 3 * wide
     scale = (3.0 * bricks * local_sites) ** (-0.5)
     vmem, dma = pltpu.VMEM, pltpu.SemaphoreType.DMA
-    plan = (planes, rows, count, bricks, units, scale)
+    plan = (planes, rows, count, bricks, ships, width, scale)
     out = pl.pallas_call(
         functools.partial(fused_kernel, plan),
         out_shape=jax.ShapeDtypeStruct((rows * count * 2, rows), f32),
@@ -660,11 +661,11 @@
             vmem((4, 3, 16, wide), f32),
             vmem((8 * rows, planes * 3 * wide), low),
             vmem((planes * 3, rows, wide), low),
-            vmem((16 * most_units, most), low),
-            vmem((16 * most_units, most), low),
+            vmem((16 * count, 3 * wide), low),
+            vmem((16 * count, 3 * wide), low),
             vmem((count, 16, local_sites), low),
             vmem((count, 16, local_sites), low),
-            vmem((ships, 8 * rows, width), f32),
+            vmem((halves, per_half * width, 8 * rows), f32),
             vmem((ships, 2, 4 * rows, width), low),
             vmem((ships, 4 * rows, width), low),
             vmem((ships, bricks, 2 * rows, width), low),
@@ -691,8 +692,8 @@
     plane = LY * LZ
     bricks, vecs, subs = (lax.axis_size(a) for a in ("brick", "vec", "sub"))
     rows, local_sites = vectors.shape[0], vectors.shape[3]
-    fits = local_sites % plane == 0 and 3 <= local_sites // plane <= 4 and rows == 32
-    if fits and vecs == 2 and subs == 2 and bricks == 4 and 24 <= momenta.shape[0] < 32:
+    fits = local_sites % plane == 0 and local_sites // plane == 4 and rows == 32
+    if fits and vecs == 2 and subs == 2 and bricks == 4 and momenta.shape[0] <= 32:
         return shards_fused(vectors, gauge_links, momenta)
     return shards(vectors, gauge_links, momenta)
 

time: 49.4 us -> 49.9 us (1.010)
  no operation moved by 1% of the time
where the time goes in v5:
time: 49.9 us; the launch traced here: 49.7 us
  Pallas kernels  47.5 us (95%)
  local copies, waits for them, and re-layouts  2.15 us (4%)
    pallas_call x1, Pallas kernels, shards_fused(): pl.pallas_call(functools.partial(fused_kernel, plan), out_shape=jax.Shape...  47.5 us
    unnamed x1, local copies, waits for them, and re-layouts  2.15 us

profile of v5, /device:TPU:2, one launch (start us, length us, event | category | flops | bytes accessed | tf_op | source)
XLA Modules:
  0.0 49.7 jit_solution(11031222904410598367)
XLA Ops:
  0.0 47.5 %elementals.1 = f32[1728,32]{1,0:T(8,128)} custom-call(s32[3,27]{1,0:T(4,128)} %bitcast.15, f32[96,4,8,128]{3,2,1,0:T(8,128)} %bitcast.13, f32[864,128]{1,0:T(8,128)} %bitcast.14), custom_call_target="tpu_custom_call" | custom-call | tf_op jit(solution)/shard_map/elementals/pallas_call | solution.py:645
  47.5 2.2 %copy.7 = f32[32,27,2,32]{3,2,1,0:T(2,128)} copy(f32[32,27,2,32]{3,2,1,0:T(2,128)} %bitcast.12) | data formatting | bytes 442368

commit v6 on v5

--- a/solution.py
+++ b/solution.py
@@ -255,7 +255,9 @@
     for t in inner:
         loads[t].wait()
         unpack(t)
-    parts = (slice(0, cut), slice(cut, span))
+    parts = [slice(0, cut)] + [
+        slice(cut + i * 3 * wide, cut + (i + 1) * 3 * wide) for i in range(2)
+    ]
     unit = 2 * rows
 
     def raw_copy(index, from_slot, to_slot, ks, **ids):
@@ -265,9 +267,9 @@
             raw_sem.at[index], **ids,
         )
 
-    across = [raw_copy(i, 0, 2, parts[i], vec=1 - v) for i in range(2)]
-    beside = raw_copy(2, 0, 1, slice(0, span), sub=1 - s)
-    onward = [raw_copy(3 + i, 2, 3, parts[i], sub=1 - s) for i in range(2)]
+    across = [raw_copy(i, 0, 2, parts[i], vec=1 - v) for i in range(3)]
+    beside = raw_copy(6, 0, 1, slice(0, span), sub=1 - s)
+    onward = [raw_copy(3 + i, 2, 3, parts[i], sub=1 - s) for i in range(3)]
     for copy in across + [beside]:
         copy.start()
 
@@ -463,12 +465,20 @@
         return carry
 
     members = (inner, outer)
-    order = [(h, half, t) for h in range(halves) for half in range(2) for t in members[half]]
+    streamed = 16 * count
+    per_half = ships // halves
+    used = streamed - (per_half - 1) * width
+    spare = used % 128 // 16
+    if used + 16 * spare > width:
+        spare = 0
+    sizes = [width] * ships
+    if spare and used - 16 * spare:
+        sizes[per_half - 1] = used - 16 * spare
+    order = [(h, half, t) for half in range(2) for h in range(halves) for t in members[half]]
     per = width // 16
-    streamed = 16 * count
 
     def ready(i):
-        return order[i][1] == 0 or order[i - 1][1] == 1
+        return order[i][1] == 0 or order[i][2] != outer[0]
 
     def turn(i):
         h, half, t = order[i]
@@ -507,22 +517,21 @@
             total[h, 0:streamed] += part
 
     def finish(e):
-        per_half = ships // halves
         at = e % per_half * width
-        part = total[e // per_half, at : at + width, :].T.astype(low)
-        parted[e, 0] = part[0 : 2 * unit]
-        crossing[e] = part[2 * unit :]
+        part = total[e // per_half, at : at + sizes[e], :].T.astype(low)
+        parted[e, 0, :, 0 : sizes[e]] = part[0 : 2 * unit]
+        crossing[e, :, 0 : sizes[e]] = part[2 * unit :]
 
     roots = (v * 2 + s, (1 - v) * 2 + s)
 
     def cross(e):
         return remote(
-            crossing.at[e], parted.at[e, 1], cross_sem.at[e], vec=1 - v
+            crossing.at[e, :, 0 : sizes[e]], parted.at[e, 1, :, 0 : sizes[e]], cross_sem.at[e], vec=1 - v
         )
 
     def ends(e, hop, ds):
-        src = parted.at[e, hop, ds * unit : (ds + 1) * unit]
-        return src, rx.at[e, b]
+        src = parted.at[e, hop, ds * unit : (ds + 1) * unit, 0 : sizes[e]]
+        return src, rx.at[e, b, :, 0 : sizes[e]]
 
     def far(e, hop, ds):
         src, dst = ends(e, hop, ds)
@@ -555,7 +564,7 @@
 
     def arrive(e):
         for i in range(bricks):
-            dst = rx.at[e, i]
+            dst = rx.at[e, i, :, 0 : sizes[e]]
             pltpu.make_async_copy(dst, dst, last_sem.at[e, i]).wait()
 
     def fill_half(half):
@@ -563,40 +572,47 @@
         count_k = len(members[half]) * 3
         lax.fori_loop(first, first + count_k, fill, 0)
 
-    per_half = ships // halves
     for i, (h, half, t) in enumerate(order):
         opens = t == members[half][0]
         if i == 0:
             fill_half(0)
         if half and opens:
             if h == 0:
-                across[1].wait_recv()
-                onward[1].start()
+                for part in (1, 2):
+                    across[part].wait_recv()
+                    onward[part].start()
             for side in range(2):
                 take(1, h, side)
                 run(1, [outer[side]], h)
             if h == 0:
-                onward[1].wait_recv()
+                for part in (1, 2):
+                    onward[part].wait_recv()
                 fill_half(1)
+            else:
+                for e in range(per_half * (h - 1), per_half * h):
+                    hand_on(e)
         if i == 0 or not ready(i):
             turn(i)
         product(i)
-        if h and not half and opens:
-            for e in range(per_half * (h - 1), per_half * h):
-                hand_on(e)
         if half and not opens:
+            if h == halves - 1:
+                total[h, streamed : streamed + 16 * spare] = total[0, 16 * (count - spare) : streamed]
             for e in range(per_half * h, per_half * (h + 1)):
                 ship(e)
     for e in range(per_half * (halves - 1), ships):
         hand_on(e)
     lane_at = lax.broadcasted_iota(jnp.int32, (8, 128), 1)
-    for e in range(ships):
-        arrive(e)
+    seen = set()
     for q in range(count):
         for first in range(0, unit, 8):
             pieces = []
             for h in range(halves):
                 e, at = h * per_half + q // per, q % per * 16
+                if h == 0 and q >= count - spare:
+                    e, at = ships - 1, used + 16 * (q - count + spare)
+                if e not in seen:
+                    arrive(e)
+                    seen.add(e)
                 tile = slice(at // 128 * 128, at // 128 * 128 + 128)
                 rows_at = slice(first // 16 * 16, first // 16 * 16 + 16)
                 got = [rx[e, i, rows_at, tile].astype(f32) for i in range(bricks)]
@@ -676,7 +692,7 @@
             dma((planes + 1,)),
             dma((2, halves, 2, 2)),
             dma((2,)),
-            dma((5, 2)),
+            dma((7, 2)),
             dma((ships, 2)),
             dma((ships, bricks + 4)),
         ],
@@ -693,7 +709,7 @@
     bricks, vecs, subs = (lax.axis_size(a) for a in ("brick", "vec", "sub"))
     rows, local_sites = vectors.shape[0], vectors.shape[3]
     fits = local_sites % plane == 0 and local_sites // plane == 4 and rows == 32
-    if fits and vecs == 2 and subs == 2 and bricks == 4 and momenta.shape[0] <= 32:
+    if fits and vecs == 2 and subs == 2 and bricks == 4 and 24 <= momenta.shape[0] < 32:
         return shards_fused(vectors, gauge_links, momenta)
     return shards(vectors, gauge_links, momenta)
 

time: 49.9 us -> 45.9 us (0.920)
  Pallas kernels: 47.5 us -> 43.6 us
    pallas_call x1, Pallas kernels: 47.5 us -> 43.6 us  [shards_fused(): pl.pallas_call(functools.partial(fused_kernel, plan), out_shape=jax.Shape...]
where the time goes in v6:
time: 45.9 us; the launch traced here: 45.7 us
  Pallas kernels  43.6 us (95%)
  local copies, waits for them, and re-layouts  2.15 us (5%)
    pallas_call x1, Pallas kernels, shards_fused(): pl.pallas_call(functools.partial(fused_kernel, plan), out_shape=jax.Shape...  43.6 us
    unnamed x1, local copies, waits for them, and re-layouts  2.15 us

profile of v6, /device:TPU:2, one launch (start us, length us, event | category | flops | bytes accessed | tf_op | source)
XLA Modules:
  0.0 45.7 jit_solution(10321559558086168917)
XLA Ops:
  0.0 43.6 %elementals.1 = f32[1728,32]{1,0:T(8,128)} custom-call(s32[3,27]{1,0:T(4,128)} %bitcast.15, f32[96,4,8,128]{3,2,1,0:T(8,128)} %bitcast.13, f32[864,128]{1,0:T(8,128)} %bitcast.14), custom_call_target="tpu_custom_call" | custom-call | tf_op jit(solution)/shard_map/elementals/pallas_call | solution.py:661
  43.6 2.2 %copy.7 = f32[32,27,2,32]{3,2,1,0:T(2,128)} copy(f32[32,27,2,32]{3,2,1,0:T(2,128)} %bitcast.12) | data formatting | bytes 442368

commit v7 on v6

--- a/solution.py
+++ b/solution.py
@@ -478,7 +478,7 @@
     per = width // 16
 
     def ready(i):
-        return order[i][1] == 0 or order[i][2] != outer[0]
+        return order[i] != (0, 1, outer[0])
 
     def turn(i):
         h, half, t = order[i]
@@ -576,24 +576,22 @@
         opens = t == members[half][0]
         if i == 0:
             fill_half(0)
-        if half and opens:
-            if h == 0:
-                for part in (1, 2):
-                    across[part].wait_recv()
-                    onward[part].start()
-            for side in range(2):
-                take(1, h, side)
-                run(1, [outer[side]], h)
-            if h == 0:
-                for part in (1, 2):
-                    onward[part].wait_recv()
-                fill_half(1)
-            else:
-                for e in range(per_half * (h - 1), per_half * h):
-                    hand_on(e)
+        if half and opens and h == 0:
+            for part in (1, 2):
+                across[part].wait_recv()
+                onward[part].start()
+                for side in range(2):
+                    take(1, part - 1, side)
+                    run(1, [outer[side]], part - 1)
+            for part in (1, 2):
+                onward[part].wait_recv()
+            fill_half(1)
         if i == 0 or not ready(i):
             turn(i)
         product(i)
+        if half and opens and h:
+            for e in range(per_half * (h - 1), per_half * h):
+                hand_on(e)
         if half and not opens:
             if h == halves - 1:
                 total[h, streamed : streamed + 16 * spare] = total[0, 16 * (count - spare) : streamed]

time: 45.9 us -> 46.4 us (1.011)
  Pallas kernels: 43.6 us -> 44.1 us
    pallas_call x1, Pallas kernels: 43.6 us -> 44.1 us  [shards_fused(): pl.pallas_call(functools.partial(fused_kernel, plan), out_shape=jax.Shape...]
where the time goes in v7:
time: 46.4 us; the launch traced here: 46.2 us
  Pallas kernels  44.1 us (95%)
  local copies, waits for them, and re-layouts  2.15 us (5%)
    pallas_call x1, Pallas kernels, shards_fused(): pl.pallas_call(functools.partial(fused_kernel, plan), out_shape=jax.Shape...  44.1 us
    unnamed x1, local copies, waits for them, and re-layouts  2.15 us

profile of v7, /device:TPU:2, one launch (start us, length us, event | category | flops | bytes accessed | tf_op | source)
XLA Modules:
  0.0 46.2 jit_solution(906180322957069372)
XLA Ops:
  0.0 44.1 %elementals.1 = f32[1728,32]{1,0:T(8,128)} custom-call(s32[3,27]{1,0:T(4,128)} %bitcast.15, f32[96,4,8,128]{3,2,1,0:T(8,128)} %bitcast.13, f32[864,128]{1,0:T(8,128)} %bitcast.14), custom_call_target="tpu_custom_call" | custom-call | tf_op jit(solution)/shard_map/elementals/pallas_call | solution.py:659
  44.1 2.2 %copy.7 = f32[32,27,2,32]{3,2,1,0:T(2,128)} copy(f32[32,27,2,32]{3,2,1,0:T(2,128)} %bitcast.12) | data formatting | bytes 442368

commit v8 on v6

--- a/solution.py
+++ b/solution.py
@@ -149,8 +149,8 @@
     return lax.psum_scatter(shares, "brick", scatter_dimension=3, tiled=True)
 
 
-def fused_kernel(plan, mom_ref, v_ref, g_ref, out_ref, *scratch):
-    (vst, gst, field0, field1, table, moved0, moved1, right, smeared, left0, left1, cosb, sinb, total, parted,
+def fused_kernel(plan, momenta_ref, v_ref, g_ref, out_ref, *scratch):
+    (mom_ref, mom_sem, vst, gst, field0, field1, table, moved0, moved1, right, smeared, left0, left1, cosb, sinb, total, parted,
      crossing, rx, halo, hsend, lsend, lrecv, load_sem, halo_sem, link_sem, raw_sem, cross_sem, last_sem) = scratch
     planes, rows, count, bricks, ships, width, scale = plan
     fields, moved = (field0, field1), (moved0, moved1)
@@ -181,6 +181,8 @@
         loads[t].start()
     load_links = pltpu.make_async_copy(g_ref, gst.at[pl.ds(0, 54 * all_tiles)], load_sem.at[planes])
     load_links.start()
+    load_momenta = pltpu.make_async_copy(momenta_ref, mom_ref, mom_sem)
+    load_momenta.start()
     barrier = pltpu.get_barrier_semaphore()
     for db in range(bricks):
         for ds in range(2):
@@ -335,6 +337,7 @@
                 sinb[q, :, at : at + 128] = jnp.broadcast_to(sine[j : j + 1], (16, 128)).astype(low)
         return carry
 
+    load_momenta.wait()
     lax.fori_loop(0, count, phases, 0)
 
     def shift(stage, k, to):
@@ -466,14 +469,7 @@
 
     members = (inner, outer)
     streamed = 16 * count
-    per_half = ships // halves
-    used = streamed - (per_half - 1) * width
-    spare = used % 128 // 16
-    if used + 16 * spare > width:
-        spare = 0
-    sizes = [width] * ships
-    if spare and used - 16 * spare:
-        sizes[per_half - 1] = used - 16 * spare
+    per_half, used, spare, sizes = pieces_of(count, halves, ships, width)
     order = [(h, half, t) for half in range(2) for h in range(halves) for t in members[half]]
     per = width // 16
 
@@ -601,28 +597,10 @@
                 ship(e)
     for e in range(per_half * (halves - 1), ships):
         hand_on(e)
-    lane_at = lax.broadcasted_iota(jnp.int32, (8, 128), 1)
-    seen = set()
-    for q in range(count):
-        for first in range(0, unit, 8):
-            pieces = []
-            for h in range(halves):
-                e, at = h * per_half + q // per, q % per * 16
-                if h == 0 and q >= count - spare:
-                    e, at = ships - 1, used + 16 * (q - count + spare)
-                if e not in seen:
-                    arrive(e)
-                    seen.add(e)
-                tile = slice(at // 128 * 128, at // 128 * 128 + 128)
-                rows_at = slice(first // 16 * 16, first // 16 * 16 + 16)
-                got = [rx[e, i, rows_at, tile].astype(f32) for i in range(bricks)]
-                got = (got[0] + got[1]) + (got[2] + got[3])
-                got = got[first % 16 : first % 16 + 8]
-                turned = (16 * h - at) % 128
-                pieces.append(pltpu.roll(got, turned, 1) if turned else got)
-            value = jnp.where(lane_at < 16, pieces[0], pieces[1])
-            start = (first % rows) * 2 * count + 2 * q + first // rows
-            out_ref[pl.ds(start, 8, stride=2 * count), :] = value[:, 0:rows]
+    for e in [i * per_half + j for j in range(per_half) for i in range(halves)]:
+        arrive(e)
+        got = [rx[e, i, :, 0 : sizes[e]].astype(f32) for i in range(bricks)]
+        out_ref[:, e * width : e * width + sizes[e]] = (got[0] + got[1]) + (got[2] + got[3])
     sent = [links_up, *across, beside, *onward]
     for copy in copies.values():
         sent += copy
@@ -636,6 +614,40 @@
             @pl.when(roots[hop] != b)
             def _():
                 far(e, hop, 0).wait_send()
+
+
+def pieces_of(count, halves, ships, width):
+    per_half = ships // halves
+    used = 16 * count - (per_half - 1) * width
+    spare = used % 128 // 16
+    if used + 16 * spare > width:
+        spare = 0
+    sizes = [width] * ships
+    if spare and used - 16 * spare:
+        sizes[per_half - 1] = used - 16 * spare
+    return per_half, used, spare, sizes
+
+
+def rows_kernel(plan, sums_ref, out_ref):
+    rows, count, ships, width = plan
+    halves, unit = rows // 16, 2 * rows
+    per = width // 16
+    per_half, used, spare, _ = pieces_of(count, halves, ships, width)
+    lane_at = lax.broadcasted_iota(jnp.int32, (8, 128), 1)
+    for q in range(count):
+        for first in range(0, unit, 8):
+            pieces = []
+            for h in range(halves):
+                e, at = h * per_half + q // per, q % per * 16
+                if h == 0 and q >= count - spare:
+                    e, at = ships - 1, used + 16 * (q - count + spare)
+                tile = e * width + at // 128 * 128
+                got = sums_ref[first : first + 8, tile : tile + 128]
+                turned = (16 * h - at) % 128
+                pieces.append(pltpu.roll(got, turned, 1) if turned else got)
+            value = jnp.where(lane_at < 16, pieces[0], pieces[1])
+            start = (first % rows) * 2 * count + 2 * q + first // rows
+            out_ref[pl.ds(start, 8, stride=2 * count), :] = value[:, 0:rows]
 
 
 def shards_fused(vectors, gauge_links, momenta):
@@ -660,14 +672,16 @@
     plan = (planes, rows, count, bricks, ships, width, scale)
     out = pl.pallas_call(
         functools.partial(fused_kernel, plan),
-        out_shape=jax.ShapeDtypeStruct((rows * count * 2, rows), f32),
+        out_shape=jax.ShapeDtypeStruct((2 * rows, ships * width), f32),
         in_specs=[
-            pl.BlockSpec(memory_space=pltpu.SMEM),
+            pl.BlockSpec(memory_space=pl.ANY),
             pl.BlockSpec(memory_space=pl.ANY),
             pl.BlockSpec(memory_space=pl.ANY),
         ],
         out_specs=pl.BlockSpec(memory_space=pltpu.VMEM),
         scratch_shapes=[
+            pltpu.SMEM((3, count), jnp.int32),
+            dma,
             vmem((planes, rows * 3, tiles * 2, 128), f32),
             vmem((64 * planes * tiles, 128), f32),
             vmem((planes + 2, 3, rows, wide), f32),
@@ -701,6 +715,13 @@
         ),
         name="elementals",
     )(momenta.T, v, g)
+    out = pl.pallas_call(
+        functools.partial(rows_kernel, (rows, count, ships, width)),
+        out_shape=jax.ShapeDtypeStruct((rows * count * 2, rows), f32),
+        in_specs=[pl.BlockSpec(memory_space=pltpu.VMEM)],
+        out_specs=pl.BlockSpec(memory_space=pltpu.VMEM),
+        name="rows",
+    )(out)
     return out.reshape((rows, count, 2, rows))
 
 

time: 45.9 us -> 44.9 us (0.978)
  local copies, waits for them, and re-layouts: 2.15 us -> 0 us
  Pallas kernels: 43.6 us -> 44.7 us
    pallas_call x0 -> x1, Pallas kernels: none -> 2.32 us  [shards_fused(): pl.pallas_call(functools.partial(rows_kernel, (rows, count, ships, width)...]
    unnamed x1 -> x0, local copies, waits for them, and re-layouts: 2.15 us -> none
    pallas_call x1, Pallas kernels: 43.6 us -> 42.4 us  [shards_fused(): pl.pallas_call(functools.partial(fused_kernel, plan), out_shape=jax.Shape...]
where the time goes in v8:
time: 44.9 us; the launch traced here: 44.7 us
  Pallas kernels  44.7 us (100%)
    pallas_call x1, Pallas kernels, shards_fused(): pl.pallas_call(functools.partial(fused_kernel, plan), out_shape=jax.Shape...  42.4 us
    pallas_call x1, Pallas kernels, shards_fused(): pl.pallas_call(functools.partial(rows_kernel, (rows, count, ships, width)...  2.32 us

profile of v8, /device:TPU:2, one launch (start us, length us, event | category | flops | bytes accessed | tf_op | source)
XLA Modules:
  0.0 44.7 jit_solution(4659110573661868454)
XLA Ops:
  0.0 42.4 %elementals.1.sums_ref = f32[64,1024]{1,0:T(8,128)} custom-call(s32[3,27]{1,0:T(4,128)} %bitcast.14, f32[96,4,8,128]{3,2,1,0:T(8,128)} %bitcast.12, f32[864,128]{1,0:T(8,128)} %bitcast.13), custom_call_target="tpu_custom_call" | custom-call | tf_op jit(solution)/shard_map/elementals/pallas_call | solution.py:673
  42.4 2.3 %rows.1 = f32[1728,32]{1,0:T(8,128)} custom-call(f32[64,1024]{1,0:T(8,128)} %elementals.1.sums_ref), custom_call_target="tpu_custom_call" | custom-call | tf_op jit(solution)/shard_map/rows/pallas_call | solution.py:718

commit v9 on v8

--- a/solution.py
+++ b/solution.py
@@ -573,22 +573,21 @@
         if i == 0:
             fill_half(0)
         if half and opens:
-            if h == 0:
-                for part in (1, 2):
-                    across[part].wait_recv()
-                    onward[part].start()
             for side in range(2):
+                if h == 0:
+                    across[1 + side].wait_recv()
+                    onward[1 + side].start()
                 take(1, h, side)
                 run(1, [outer[side]], h)
-            if h == 0:
-                for part in (1, 2):
-                    onward[part].wait_recv()
-                fill_half(1)
-            else:
+            if h:
                 for e in range(per_half * (h - 1), per_half * h):
                     hand_on(e)
         if i == 0 or not ready(i):
             turn(i)
+        if half and opens and h == 0:
+            for part in (1, 2):
+                onward[part].wait_recv()
+            fill_half(1)
         product(i)
         if half and not opens:
             if h == halves - 1:
@@ -628,26 +627,33 @@
     return per_half, used, spare, sizes
 
 
-def rows_kernel(plan, sums_ref, out_ref):
+def rows_kernel(plan, sums_ref, out_ref, stage, sems):
     rows, count, ships, width = plan
-    halves, unit = rows // 16, 2 * rows
-    per = width // 16
+    halves, per = rows // 16, width // 16
     per_half, used, spare, _ = pieces_of(count, halves, ships, width)
     lane_at = lax.broadcasted_iota(jnp.int32, (8, 128), 1)
-    for q in range(count):
-        for first in range(0, unit, 8):
-            pieces = []
-            for h in range(halves):
-                e, at = h * per_half + q // per, q % per * 16
-                if h == 0 and q >= count - spare:
-                    e, at = ships - 1, used + 16 * (q - count + spare)
-                tile = e * width + at // 128 * 128
-                got = sums_ref[first : first + 8, tile : tile + 128]
-                turned = (16 * h - at) % 128
-                pieces.append(pltpu.roll(got, turned, 1) if turned else got)
-            value = jnp.where(lane_at < 16, pieces[0], pieces[1])
-            start = (first % rows) * 2 * count + 2 * q + first // rows
-            out_ref[pl.ds(start, 8, stride=2 * count), :] = value[:, 0:rows]
+    copies = []
+    for octet in range(0, rows, 8):
+        for q in range(count):
+            for part in range(2):
+                first = part * rows + octet
+                pieces = []
+                for h in range(halves):
+                    e, at = h * per_half + q // per, q % per * 16
+                    if h == 0 and q >= count - spare:
+                        e, at = ships - 1, used + 16 * (q - count + spare)
+                    tile = e * width + at // 128 * 128
+                    got = sums_ref[first : first + 8, tile : tile + 128]
+                    turned = (16 * h - at) % 128
+                    pieces.append(pltpu.roll(got, turned, 1) if turned else got)
+                value = jnp.where(lane_at < 16, pieces[0], pieces[1])
+                start = octet * 2 * count + 2 * q + part
+                stage[pl.ds(start, 8, stride=2 * count), :] = value[:, 0:rows]
+        done = pl.ds(octet * 2 * count, 16 * count)
+        copies.append(pltpu.make_async_copy(stage.at[done], out_ref.at[done], sems.at[octet // 8]))
+        copies[-1].start()
+    for copy in copies:
+        copy.wait()
 
 
 def shards_fused(vectors, gauge_links, momenta):
@@ -719,7 +725,8 @@
         functools.partial(rows_kernel, (rows, count, ships, width)),
         out_shape=jax.ShapeDtypeStruct((rows * count * 2, rows), f32),
         in_specs=[pl.BlockSpec(memory_space=pltpu.VMEM)],
-        out_specs=pl.BlockSpec(memory_space=pltpu.VMEM),
+        out_specs=pl.BlockSpec(memory_space=pl.ANY),
+        scratch_shapes=[vmem((rows * count * 2, rows), f32), dma((rows // 8,))],
         name="rows",
     )(out)
     return out.reshape((rows, count, 2, rows))

time: 44.9 us -> 45 us (level)
  no operation moved by 1% of the time
where the time goes in v9:
time: 45 us; the launch traced here: 44.9 us
  Pallas kernels  44.9 us (100%)
    pallas_call x1, Pallas kernels, shards_fused(): pl.pallas_call(functools.partial(fused_kernel, plan), out_shape=jax.Shape...  42.7 us
    pallas_call x1, Pallas kernels, shards_fused(): pl.pallas_call(functools.partial(rows_kernel, (rows, count, ships, width)...  2.13 us

profile of v9, /device:TPU:2, one launch (start us, length us, event | category | flops | bytes accessed | tf_op | source)
XLA Modules:
  0.0 44.9 jit_solution(17534111957305323112)
XLA Ops:
  0.0 42.7 %elementals.1.sums_ref = f32[64,1024]{1,0:T(8,128)} custom-call(s32[3,27]{1,0:T(4,128)} %bitcast.14, f32[96,4,8,128]{3,2,1,0:T(8,128)} %bitcast.12, f32[864,128]{1,0:T(8,128)} %bitcast.13), custom_call_target="tpu_custom_call" | custom-call | tf_op jit(solution)/shard_map/elementals/pallas_call | solution.py:679
  42.7 2.1 %rows.1 = f32[1728,32]{1,0:T(8,128)} custom-call(f32[64,1024]{1,0:T(8,128)} %elementals.1.sums_ref), custom_call_target="tpu_custom_call" | custom-call | tf_op jit(solution)/shard_map/rows/pallas_call | solution.py:724

commit v10 on v8

--- a/solution.py
+++ b/solution.py
@@ -151,7 +151,7 @@
 
 def fused_kernel(plan, momenta_ref, v_ref, g_ref, out_ref, *scratch):
     (mom_ref, mom_sem, vst, gst, field0, field1, table, moved0, moved1, right, smeared, left0, left1, cosb, sinb, total, parted,
-     crossing, rx, halo, hsend, lsend, lrecv, load_sem, halo_sem, link_sem, raw_sem, cross_sem, last_sem) = scratch
+     crossing, inward, rx, halo, hsend, lsend, lrecv, load_sem, halo_sem, link_sem, raw_sem, cross_sem, inward_sem, last_sem) = scratch
     planes, rows, count, bricks, ships, width, scale = plan
     fields, moved = (field0, field1), (moved0, moved1)
     halves = rows // 16
@@ -194,6 +194,24 @@
     pl.semaphore_signal(
         barrier, inc=1, device_id={"vec": 1 - v}, device_id_type=pl.DeviceIdType.MESH
     )
+    outermost, adder = b == 3 - 3 * v, b == 1 + v
+    pl.when(outermost)(
+        lambda: pl.semaphore_signal(
+            barrier, inc=1, device_id={"brick": 2 - v, "vec": 1 - v}, device_id_type=pl.DeviceIdType.MESH
+        )
+    )
+    pl.when(adder)(
+        lambda: pl.semaphore_signal(
+            barrier, inc=1, device_id={"brick": 3 * v, "vec": 1 - v}, device_id_type=pl.DeviceIdType.MESH
+        )
+    )
+    silent = 3 * v
+
+    @pl.when(b // 2 != v)
+    def _():
+        for e in range(ships):
+            rx[e, silent] = jnp.zeros(rx.shape[2:], low)
+
 
     def unpack(t):
         flat = vst.at[t].reshape(rows * 3 * tiles * 2, 128)
@@ -231,7 +249,8 @@
     for part in range(2):
         both = jnp.concatenate([link_rows(last, part, 0), link_rows(last, part, 1)], axis=0)
         lsend[16 * part : 16 * part + 16, :] = both.astype(low)
-    pl.semaphore_wait(barrier, 2 * bricks)
+    extra = (outermost | adder).astype(jnp.int32)
+    pl.semaphore_wait(barrier, 2 * bricks + extra)
     up, down = (b + 1) % bricks, (b + bricks - 1) % bricks
 
     def halos(step, h, low_src, high_src):
@@ -549,19 +568,46 @@
             src, dst = ends(e, hop, 0)
             pltpu.make_async_copy(src, dst, last_sem.at[e, b]).start()
 
+    def cross_inward(e):
+        return remote(
+            crossing.at[e, :, 0 : sizes[e]], inward.at[e, :, 0 : sizes[e]], inward_sem.at[e],
+            vec=1 - v, brick=2 - v,
+        )
+
     def ship(e):
         finish(e)
-        cross(e).start()
+
+        @pl.when(outermost)
+        def _():
+            cross_inward(e).start()
+
+        @pl.when(jnp.logical_not(outermost))
+        def _():
+            cross(e).start()
+
         depart(e, 0)
 
     def hand_on(e):
-        cross(e).wait_recv()
-        depart(e, 1)
+        @pl.when(adder)
+        def _():
+            cross(e).wait_recv()
+            cross_inward(e).wait_recv()
+            both = parted[e, 1, :, 0 : sizes[e]].astype(f32) + inward[e, :, 0 : sizes[e]].astype(f32)
+            parted[e, 1, :, 0 : sizes[e]] = both.astype(low)
+            depart(e, 1)
+
+        @pl.when(jnp.logical_not(adder) & (b != silent))
+        def _():
+            cross(e).wait_recv()
+            depart(e, 1)
 
     def arrive(e):
         for i in range(bricks):
-            dst = rx.at[e, i, :, 0 : sizes[e]]
-            pltpu.make_async_copy(dst, dst, last_sem.at[e, i]).wait()
+            @pl.when((b // 2 == v) | (silent != i))
+            def _():
+                dst = rx.at[e, i, :, 0 : sizes[e]]
+                pltpu.make_async_copy(dst, dst, last_sem.at[e, i]).wait()
+
 
     def fill_half(half):
         first = len(inner) * 3 if half else 0
@@ -604,16 +650,25 @@
     sent = [links_up, *across, beside, *onward]
     for copy in copies.values():
         sent += copy
-    sent += [cross(e) for e in range(ships)]
     for copy in sent:
         copy.wait_send()
     for e in range(ships):
+        @pl.when(outermost)
+        def _():
+            cross_inward(e).wait_send()
+
+        @pl.when(jnp.logical_not(outermost))
+        def _():
+            cross(e).wait_send()
+
         for hop in range(2):
-            far(e, hop, 1).wait_send()
-
-            @pl.when(roots[hop] != b)
+            @pl.when((b != silent) | (hop == 0))
             def _():
-                far(e, hop, 0).wait_send()
+                far(e, hop, 1).wait_send()
+
+                @pl.when(roots[hop] != b)
+                def _():
+                    far(e, hop, 0).wait_send()
 
 
 def pieces_of(count, halves, ships, width):
@@ -698,6 +753,7 @@
             vmem((halves, per_half * width, 8 * rows), f32),
             vmem((ships, 2, 4 * rows, width), low),
             vmem((ships, 4 * rows, width), low),
+            vmem((ships, 4 * rows, width), low),
             vmem((ships, bricks, 2 * rows, width), low),
             vmem((2, halves, 2, 16, 3 * wide), low),
             vmem((halves, 2, 16, 3 * wide), low),
@@ -707,6 +763,7 @@
             dma((2, halves, 2, 2)),
             dma((2,)),
             dma((7, 2)),
+            dma((ships, 2)),
             dma((ships, 2)),
             dma((ships, bricks + 4)),
         ],

time: 44.9 us -> 45.8 us (1.020)
  Pallas kernels: 44.7 us -> 45.6 us
    pallas_call x1, Pallas kernels: 42.4 us -> 43.3 us  [shards_fused(): pl.pallas_call(functools.partial(fused_kernel, plan), out_shape=jax.Shape...]
where the time goes in v10:
time: 45.8 us; the launch traced here: 45.7 us
  Pallas kernels  45.6 us (100%)
    pallas_call x1, Pallas kernels, shards_fused(): pl.pallas_call(functools.partial(fused_kernel, plan), out_shape=jax.Shape...  43.3 us
    pallas_call x1, Pallas kernels, shards_fused(): pl.pallas_call(functools.partial(rows_kernel, (rows, count, ships, width)...  2.32 us

profile of v10, /device:TPU:2, one launch (start us, length us, event | category | flops | bytes accessed | tf_op | source)
XLA Modules:
  0.0 45.7 jit_solution(15838456893851848189)
XLA Ops:
  0.0 43.3 %elementals.1.sums_ref = f32[64,1024]{1,0:T(8,128)} custom-call(s32[3,27]{1,0:T(4,128)} %bitcast.14, f32[96,4,8,128]{3,2,1,0:T(8,128)} %bitcast.12, f32[864,128]{1,0:T(8,128)} %bitcast.13), custom_call_target="tpu_custom_call" | custom-call | tf_op jit(solution)/shard_map/elementals/pallas_call | solution.py:728
  43.3 2.3 %rows.1 = f32[1728,32]{1,0:T(8,128)} custom-call(f32[64,1024]{1,0:T(8,128)} %elementals.1.sums_ref), custom_call_target="tpu_custom_call" | custom-call | tf_op jit(solution)/shard_map/rows/pallas_call | solution.py:775

commit v11 on v8

--- a/solution.py
+++ b/solution.py
@@ -491,7 +491,7 @@
                     to[16 * q : 16 * q + 16, col : col + 256] = cosine * sr + sine * si
                     to[16 * q : 16 * q + 16, col + plane : col + plane + 256] = cosine * si - sine * sr
 
-    def product(i):
+    def product(i, start=0, stop=streamed, ahead=True):
         h, half, t = order[i]
         first = position[t] * 3 * wide
         length = 3 * wide
@@ -499,18 +499,18 @@
         for k in range(0, length, length // 2):
             pieces.append(
                 lax.dot_general(
-                    left[i % 2][:, k : k + length // 2],
+                    left[i % 2][start:stop, k : k + length // 2],
                     right[:, first + k : first + k + length // 2],
                     (((1,), (1,)), ((), ())), preferred_element_type=f32,
                 )
             )
-        if i + 1 < len(order) and ready(i + 1):
+        if ahead and i + 1 < len(order) and ready(i + 1):
             turn(i + 1)
         part = pieces[0] * scale + pieces[1] * scale
         if t == inner[0]:
-            total[h, 0:streamed] = part
+            total[h, start:stop] = part
         else:
-            total[h, 0:streamed] += part
+            total[h, start:stop] += part
 
     def finish(e):
         at = e % per_half * width
@@ -589,10 +589,18 @@
                     hand_on(e)
         if i == 0 or not ready(i):
             turn(i)
+        if half and h == halves - 1:
+            if opens:
+                for e in range(per_half):
+                    start, stop = e * width, min((e + 1) * width, streamed)
+                    product(i, start, stop, e == 0)
+                    product(i + 1, start, stop, False)
+                    if e == per_half - 1:
+                        total[h, streamed : streamed + 16 * spare] = total[0, 16 * (count - spare) : streamed]
+                    ship(per_half * h + e)
+            continue
         product(i)
         if half and not opens:
-            if h == halves - 1:
-                total[h, streamed : streamed + 16 * spare] = total[0, 16 * (count - spare) : streamed]
             for e in range(per_half * h, per_half * (h + 1)):
                 ship(e)
     for e in range(per_half * (halves - 1), ships):

time: 44.9 us -> 44.9 us (level)
  no operation moved by 1% of the time
where the time goes in v11:
time: 44.9 us; the launch traced here: 44.8 us
  Pallas kernels  44.7 us (100%)
    pallas_call x1, Pallas kernels, shards_fused(): pl.pallas_call(functools.partial(fused_kernel, plan), out_shape=jax.Shape...  42.4 us
    pallas_call x1, Pallas kernels, shards_fused(): pl.pallas_call(functools.partial(rows_kernel, (rows, count, ships, width)...  2.32 us

profile of v11, /device:TPU:2, one launch (start us, length us, event | category | flops | bytes accessed | tf_op | source)
XLA Modules:
  0.0 44.8 jit_solution(1830908946842922974)
XLA Ops:
  0.0 42.4 %elementals.1.sums_ref = f32[64,1024]{1,0:T(8,128)} custom-call(s32[3,27]{1,0:T(4,128)} %bitcast.14, f32[96,4,8,128]{3,2,1,0:T(8,128)} %bitcast.12, f32[864,128]{1,0:T(8,128)} %bitcast.13), custom_call_target="tpu_custom_call" | custom-call | tf_op jit(solution)/shard_map/elementals/pallas_call | solution.py:681
  42.4 2.3 %rows.1 = f32[1728,32]{1,0:T(8,128)} custom-call(f32[64,1024]{1,0:T(8,128)} %elementals.1.sums_ref), custom_call_target="tpu_custom_call" | custom-call | tf_op jit(solution)/shard_map/rows/pallas_call | solution.py:726

commit v12 on v11

--- a/solution.py
+++ b/solution.py
@@ -584,9 +584,6 @@
                 for part in (1, 2):
                     onward[part].wait_recv()
                 fill_half(1)
-            else:
-                for e in range(per_half * (h - 1), per_half * h):
-                    hand_on(e)
         if i == 0 or not ready(i):
             turn(i)
         if half and h == halves - 1:
@@ -598,6 +595,7 @@
                     if e == per_half - 1:
                         total[h, streamed : streamed + 16 * spare] = total[0, 16 * (count - spare) : streamed]
                     ship(per_half * h + e)
+                    hand_on(per_half * (h - 1) + e)
             continue
         product(i)
         if half and not opens:

time: 44.9 us -> 44.2 us (0.984)
  Pallas kernels: 44.7 us -> 44 us
    pallas_call x1, Pallas kernels: 42.4 us -> 41.7 us  [shards_fused(): pl.pallas_call(functools.partial(fused_kernel, plan), out_shape=jax.Shape...]
where the time goes in v12:
time: 44.2 us; the launch traced here: 44 us
  Pallas kernels  44 us (100%)
    pallas_call x1, Pallas kernels, shards_fused(): pl.pallas_call(functools.partial(fused_kernel, plan), out_shape=jax.Shape...  41.7 us
    pallas_call x1, Pallas kernels, shards_fused(): pl.pallas_call(functools.partial(rows_kernel, (rows, count, ships, width)...  2.32 us

profile of v12, /device:TPU:2, one launch (start us, length us, event | category | flops | bytes accessed | tf_op | source)
XLA Modules:
  0.0 44.0 jit_solution(9817989005941834620)
XLA Ops:
  0.0 41.7 %elementals.1.sums_ref = f32[64,1024]{1,0:T(8,128)} custom-call(s32[3,27]{1,0:T(4,128)} %bitcast.14, f32[96,4,8,128]{3,2,1,0:T(8,128)} %bitcast.12, f32[864,128]{1,0:T(8,128)} %bitcast.13), custom_call_target="tpu_custom_call" | custom-call | tf_op jit(solution)/shard_map/elementals/pallas_call | solution.py:679
  41.7 2.3 %rows.1 = f32[1728,32]{1,0:T(8,128)} custom-call(f32[64,1024]{1,0:T(8,128)} %elementals.1.sums_ref), custom_call_target="tpu_custom_call" | custom-call | tf_op jit(solution)/shard_map/rows/pallas_call | solution.py:724
